TPU v7x, 32 devices: a whole 2x2x4 slice. The times are simulated.
32 devices in a mesh: expert: 16 (over z, y, x), tensor: 2 (over core).
Axes of the slice: x: 2, y: 2, z: 4, core: 2. Of those that a mesh axis runs over, the one named last changes fastest.
Arguments:
- tokens: bfloat16 [1024, 5120], P('expert', 'tensor'), may hold values from -6 to 6
- w_gate: bfloat16 [16, 5120, 1536], P('expert', None, 'tensor'), may hold values from -0.078125 to 0.078125
- w_up: bfloat16 [16, 5120, 1536], P('expert', None, 'tensor'), may hold values from -0.078125 to 0.078125
- w_down: bfloat16 [16, 1536, 5120], P('expert', 'tensor'), may hold values from -0.15625 to 0.15625
- route_ids: int32 [1024, 6], P('expert'), may hold values from 0 to 15, all different within a row; in each aligned block of 64 rows (0 to 63, 64 to 127, ...) at most 36 rows name the same one
- route_weight: float32 [1024, 6], P('expert'), may hold values from 0.1 to 1
- live_count: int32 [16], P('expert'), may hold values from 32 to 64, as said below
- owner_slot: int32 [1024], P('expert'), may hold values from 0 to 63, as said below
Outputs:
- mixed: bfloat16 [1024, 5120], P('expert', 'tensor')
Inputs may be any that keep to these rules, and one draw needn't show every extreme that they name: `route_ids`: each row names 6 different experts; among the 64 rows of one index of expert no expert is named by more than 36 rows, and in some index one expert is named by exactly 36. `live_count`: a multiple of 16; some index of expert has all 64 slots live. `owner_slot`: within the 64 rows of each index of expert, each of 0 to 63 once.
All inputs are finite; a program needn't handle non-finite values.
Results may differ from a plain program's by a relative error of at most 0.0057.
Values may be sent and summed in bfloat16 or wider, within the bound.
No kernel may reach another device: no remote copies, remote signals or barrier semaphores. Data moves between devices by JAX's collectives and lax.ppermute only.
A program may use at most 128 MiB of HBM per device.

v0:
```python
import jax
import jax.numpy as jnp
from jax import lax
from jax.sharding import PartitionSpec as P


def body(tokens, w_gate, w_up, w_down, route_ids, route_weight, live_count, owner_slot):
    tok_dev, top = route_ids.shape
    groups = lax.axis_size("expert")
    capacity = 3 * tok_dev * top // (2 * groups)
    slots = groups * capacity
    live = jnp.arange(tok_dev, dtype=jnp.int32) < live_count[0]
    flat_expert = route_ids.reshape(-1)
    hits = (flat_expert[:, None] == jnp.arange(groups, dtype=jnp.int32)[None, :]).astype(jnp.int32)
    before = jnp.cumsum(hits, 0) - hits
    ranking = jnp.sum(before * hits, 1)
    target = flat_expert * capacity + ranking
    valid = jnp.repeat(live, top)
    chosen = (jnp.arange(slots, dtype=jnp.int32)[:, None] == target[None, :]) & valid[None, :]
    dispatch = jnp.sum(chosen.reshape(slots, tok_dev, top).astype(jnp.int32), 2).astype(
        jnp.bfloat16
    )
    gate_w = w_gate[0]
    up_w = w_up[0]
    down_w = w_down[0]
    out_width = down_w.shape[1]
    outgoing = jnp.dot(dispatch, tokens, preferred_element_type=jnp.float32).astype(jnp.bfloat16)
    outgoing = outgoing.reshape(groups, capacity, tokens.shape[1])
    piece = lax.all_to_all(outgoing, "expert", split_axis=0, concat_axis=0, tiled=True)
    piece = lax.all_gather(piece, "tensor", axis=2, tiled=True)
    sources, items, width = piece.shape
    count = sources * items
    rows = piece.reshape(count, width)
    gate = jnp.dot(rows, gate_w, preferred_element_type=jnp.float32)
    up = jnp.dot(rows, up_w, preferred_element_type=jnp.float32)
    result = jnp.dot(
        (jax.nn.silu(gate) * up).astype(jnp.bfloat16), down_w, preferred_element_type=jnp.float32
    )
    summed = lax.psum_scatter(
        result.reshape(sources, items, out_width), "tensor", scatter_dimension=2, tiled=True
    )
    results = summed.astype(jnp.bfloat16)
    returned = lax.all_to_all(results, "expert", split_axis=0, concat_axis=0, tiled=True)
    returned = returned.reshape(slots, returned.shape[2])
    picked = target.reshape(tok_dev, top)[owner_slot]
    weight = jnp.where(live[owner_slot][:, None], route_weight[owner_slot], jnp.float32(0.0))
    values = (
        returned[picked.reshape(-1)].reshape(tok_dev, top, returned.shape[1]).astype(jnp.float32)
    )
    mixed = jnp.sum(values * weight[:, :, None], 1)
    return mixed.astype(jnp.bfloat16)


def solution(mesh):
    placed = (
        P("expert", "tensor"),
        P("expert", None, "tensor"),
        P("expert", None, "tensor"),
        P("expert", "tensor", None),
        P("expert", None),
        P("expert", None),
        P("expert"),
        P("expert"),
    )
    return jax.shard_map(
        body, mesh=mesh, in_specs=placed, out_specs=P("expert", "tensor"), check_vma=False
    )
```

profile of v0, /device:TPU:14, one launch (start us, length us, event | category | flops | bytes accessed | tf_op | source)
XLA Modules:
  0.0 278.9 jit_solution(2911542716467942462)
XLA Ops:
  6.5 0.8 copy.25
  7.7 0.9 reduce-window.6
  8.5 0.2 slice_reduce_fusion
  9.1 0.7 multiply_add_fusion
  10.5 0.2 convert_reduce_fusion
  10.7 0.9 convolution_convert_fusion
  11.7 2.4 reshape.107
  14.0 79.2 %all_to_all.10 = bf16[16,36,2560]{2,1,0:T(8,128)(2,1)} all-to-all(bf16[16,36,2560]{2,1,0:T(8,128)(2,1)} %reshape.107), channel_id=1, replica_groups=mesh['expert'=16,'tensor'=2] {'expert'}, dimensions={0} | all-to-all | bytes 5898240 | tf_op jit(solution)/shard_map/all_to_all | solution.py:29
  93.4 17.5 %all-gather.2.cloned.1.call-done = bf16[16,36,5120]{2,1,0:T(8,128)(2,1)} async-done(((bf16[16,36,2560]{2,1,0:T(8,128)(2,1)}), bf16[16,36,5120]{2,1,0:T(8,128)(2,1)}) %all-gather.2.cloned.1.call-update) | async-done | bytes 5898256 | tf_op jit(solution)/shard_map/all_gather | solution.py:30
  110.8 8.2 %reshape.108 = bf16[576,5120]{1,0:T(8,128)(2,1)} reshape(bf16[16,36,5120]{2,1,0:T(8,128)(2,1)} %all-gather.2.cloned.1.call-done) | data formatting | bytes 11796480 | tf_op jit(solution)/shard_map/reshape | solution.py:33
  119.0 9.4 %fusion.4 = f32[576,768]{1,0:T(8,128)S(1)} fusion(bf16[576,5120]{1,0:T(8,128)(2,1)} %reshape.108, bf16[1,5120,768]{2,1,0:T(8,128)(2,1)} %param.9), kind=kOutput, calls=%fused_computation.8 | convolution fusion | flops 4529848320 | bytes 15532032 | tf_op jit(solution)/shard_map/dot_general | solution.py:34
  128.4 8.0 %multiply_convert_fusion = bf16[576,768]{1,0:T(8,128)(2,1)S(1)} fusion(f32[576,768]{1,0:T(8,128)S(1)} %fusion.4, bf16[576,5120]{1,0:T(8,128)(2,1)S(1)} %copy-done.2, bf16[1,5120,768]{2,1,0:T(8,128)(2,1)} %param.10), kind=kOutput, calls=%fused_computation.12 | convolution fusion | flops 4532502528 | bytes 16416768 | tf_op jit(solution)/shard_map/dot_general | solution.py:35
  136.6 11.4 %fusion = f32[16,36,5120]{2,1,0:T(8,128)} fusion(bf16[16,36,768]{2,1,0:T(8,128)(2,1)S(1)} %dot_general.17, bf16[1,768,5120]{2,1,0:T(8,128)(2,1)} %param.11), kind=kOutput, calls=%fused_computation.4 | convolution fusion | flops 4529848320 | bytes 20545536 | tf_op jit(solution)/shard_map/dot_general | solution.py:36
  148.0 21.2 %reduce-scatter.2.cloned.1.call-done = f32[16,36,2560]{2,1,0:T(8,128)} async-done(((f32[16,36,5120]{2,1,0:T(8,128)}), f32[16,36,2560]{2,1,0:T(8,128)}) %reduce-scatter.2.cloned.1.call-update) | async-done | bytes 5898256 | tf_op jit(solution)/shard_map/reduce_scatter | solution.py:39
  169.3 4.9 %convert_element_type.37 = bf16[16,36,2560]{2,1,0:T(8,128)(2,1)} convert(f32[16,36,2560]{2,1,0:T(8,128)} %reduce-scatter.2.cloned.1.call-done) | non-fusion elementwise | flops 1474560 | bytes 8847360 | tf_op jit(solution)/shard_map/convert_element_type | solution.py:42
  174.2 7.1 %all-to-all-start.1 = ((bf16[16,36,2560]{2,1,0:T(8,128)(2,1)}), bf16[16,36,2560]{2,1,0:T(8,128)(2,1)}, u32[]{:S(2)}, u32[]{:S(2)}) async-start(bf16[16,36,2560]{2,1,0:T(8,128)(2,1)} %convert_element_type.37), calls=%async_computation.2 | async-start | bytes 6553600 | tf_op jit(solution)/shard_map/all_to_all | solution.py:43
  181.4 0.8 gather_fusion.2
  182.2 0.6 gather_fusion
  183.0 0.6 gather_fusion.3
  183.7 72.5 %all-to-all-done.1 = bf16[16,36,2560]{2,1,0:T(8,128)(2,1)} async-done(((bf16[16,36,2560]{2,1,0:T(8,128)(2,1)}), bf16[16,36,2560]{2,1,0:T(8,128)(2,1)}, u32[]{:S(2)}, u32[]{:S(2)}) %all-to-all-start.1) | async-done | bytes 2949152 | tf_op jit(solution)/shard_map/all_to_all | solution.py:43
  256.2 2.9 %reshape.109 = bf16[576,2560]{1,0:T(8,128)(2,1)S(1)} reshape(bf16[16,36,2560]{2,1,0:T(8,128)(2,1)} %all-to-all-done.1) | data formatting | bytes 5898240 | tf_op jit(solution)/shard_map/reshape | solution.py:44
  259.1 3.3 %gather_fusion.1 = bf16[384,2560]{1,0:T(8,128)(2,1)} fusion(bf16[576,2560]{1,0:T(8,128)(2,1)S(1)} %reshape.109, s32[1024]{0:T(1024)S(1)} %pad_clamp_fusion), kind=kCustom, calls=%fused_computation.1 | custom fusion | bytes 3933696 | tf_op jit(solution)/shard_map/gather | solution.py:48
  262.4 4.5 %reshape.111 = f32[64,6,2560]{2,1,0:T(8,128)} reshape(bf16[384,2560]{1,0:T(8,128)(2,1)} %gather_fusion.1) | data formatting | bytes 5898240 | tf_op jit(solution)/shard_map/convert_element_type | solution.py:48
  266.9 5.2 %multiply_reduce_fusion = bf16[64,2560]{1,0:T(8,128)(2,1)} fusion(f32[64,6,2560]{2,1,0:T(8,128)} %reshape.111, f32[64,6]{1,0:T(8,128)S(1)} %broadcast_select_fusion), kind=kLoop, calls=%fused_computation.10 | loop fusion | flops 1802240 | bytes 4261376 | tf_op jit(solution)/shard_map/reduce_sum | solution.py:50
  (31 shorter events, 1.3 us)
Async XLA Ops:
  6.5 4.2 %copy-start = (bf16[64,2560]{1,0:T(8,128)(2,1)S(1)}, bf16[64,2560]{1,0:T(8,128)(2,1)}, u32[]{:S(2)}) copy-start(bf16[64,2560]{1,0:T(8,128)(2,1)} %param.8) | copy-start | bytes 983044
  6.5 104.3 %all-gather.2.cloned.1.call-start = ((), (), s32[]{:S(2)}) async-start(), calls=%async_computation.3 | async-start | bytes 9830400 | tf_op jit(solution)/shard_map/all_gather | solution.py:30
  93.3 75.9 %reduce-scatter.2.cloned.1.call-start = ((), (), s32[]{:S(2)}) async-start(), calls=%async_computation.4 | async-start | bytes 19660800 | tf_op jit(solution)/shard_map/reduce_scatter | solution.py:39
  119.0 9.4 %copy-start.2 = (bf16[576,5120]{1,0:T(8,128)(2,1)S(1)}, bf16[576,5120]{1,0:T(8,128)(2,1)}, u32[]{:S(2)}) copy-start(bf16[576,5120]{1,0:T(8,128)(2,1)} %reshape.108) | copy-start | bytes 17694724
  174.2 7.2 %copy-start.4 = (s32[64]{0:T(128)S(1)}, s32[64]{0:T(128)}, u32[]{:S(2)}) copy-start(s32[64]{0:T(128)} %param.15) | copy-start | bytes 772
  174.2 8.7 %copy-start.3 = (f32[64,6]{0,1:T(8,128)S(1)}, f32[64,6]{0,1:T(8,128)}, u32[]{:S(2)}) copy-start(f32[64,6]{0,1:T(8,128)} %param.13) | copy-start | bytes 4612
  174.2 82.0 %all-to-all-start.1 = ((bf16[16,36,2560]{2,1,0:T(8,128)(2,1)}), bf16[16,36,2560]{2,1,0:T(8,128)(2,1)}, u32[]{:S(2)}, u32[]{:S(2)}) async-start(bf16[16,36,2560]{2,1,0:T(8,128)(2,1)} %convert_element_type.37), calls=%async_computation.2 | async-start | bytes 6553600 | tf_op jit(solution)/shard_map/all_to_all | solution.py:43
  259.1 12.9 %copy-start.1 = (bf16[64,2560]{1,0:T(8,128)(2,1)S(1)}, bf16[64,2560]{1,0:T(8,128)(2,1)}, u32[]{:S(2)}) copy-start(bf16[64,2560]{1,0:T(8,128)(2,1)} %param.8) | copy-start | bytes 983044
Sparse Core Ops, SparseCore 0:
  93.4 17.3 all-gather.1
  148.2 21.0 reduce-scatter.1
where the time goes:
time: 280 us; the launch traced here: 279 us
  waiting for transfers between devices  111 us (40%)
  blocking collectives  79.2 us (28%)
  matrix products  29.7 us (11%)
  local copies, waits for them, and re-layouts  25.2 us (9%)
  between operations  14.2 us (5%)
  other arithmetic  12.1 us (4%)
  starting transfers between devices  7.13 us (3%)
    all_to_all x1, blocking collectives, body(): lax.all_to_all(outgoing, 'expert', split_axis=0, concat_axis=0, tiled=True)  79.2 us
    all_to_all x1, waiting for transfers between devices, body(): lax.all_to_all(results, 'expert', split_axis=0, concat_axis=0, tiled=True)  72.5 us
    reduce_scatter x1, waiting for transfers between devices, body(): lax.psum_scatter(result.reshape(sources, items, out_width), 'tensor', sca...  21.2 us
    all_gather x1, waiting for transfers between devices, body(): piece = lax.all_gather(piece, 'tensor', axis=2, tiled=True)  17.5 us
    dot_general x1, matrix products, body(): jnp.dot((jax.nn.silu(gate) * up).astype(jnp.bfloat16), down_w, preferred_...  11.4 us
    dot_general x1, matrix products, body(): gate = jnp.dot(rows, gate_w, preferred_element_type=jnp.float32)  9.35 us
    reshape x1, local copies, waits for them, and re-layouts, body(): rows = piece.reshape(count, width)  8.16 us
    dot_general x1, matrix products, body(): up = jnp.dot(rows, up_w, preferred_element_type=jnp.float32)  8.05 us
  transfers between devices with their start and end apart: 3, of which 3 were waited for; matrix products, arithmetic and copies ran while one was open for 1% of the time, Pallas kernels for 0%

commit v1 on v0

--- a/solution.py
+++ b/solution.py
@@ -3,8 +3,11 @@
 from jax import lax
 from jax.sharding import PartitionSpec as P
 
-
-def body(tokens, w_gate, w_up, w_down, route_ids, route_weight, live_count, owner_slot):
+CHUNKS = 2
+BOTH = ("expert", "tensor")
+
+
+def exchange_body(tokens, w_gate, w_up, w_down, route_ids, route_weight, live_count, owner_slot):
     tok_dev, top = route_ids.shape
     groups = lax.axis_size("expert")
     capacity = 3 * tok_dev * top // (2 * groups)
@@ -51,7 +54,145 @@
     return mixed.astype(jnp.bfloat16)
 
 
+def block_diagonal(picks):
+    count, rows, cols = picks.shape
+    same = jnp.eye(count, dtype=picks.dtype)
+    return (picks[:, :, None, :] * same[:, None, :, None]).reshape(count * rows, count * cols)
+
+
+def tree_body(tokens, w_gate, w_up, w_down, route_ids, route_weight, live_count, owner_slot):
+    tok_dev, top = route_ids.shape
+    width = tokens.shape[1]
+    groups = lax.axis_size("expert")
+    ring = groups // 4
+    capacity = 3 * tok_dev * top // (2 * groups)
+    bf16, f32 = jnp.bfloat16, jnp.float32
+    me = lax.axis_index("expert")
+    core = lax.axis_index("tensor")
+    first = core == 0
+
+    bits = ((2, 1), (1, 2))
+    cells = [(e, c) for e in range(groups) for c in range(2)]
+
+    def turn(places):
+        return [(2 * e + c, 2 * ((e + 4 * places) % groups) + c) for e, c in cells]
+
+    near = [(2 * e + c, 2 * (e ^ bits[c][0]) + c) for e, c in cells]
+    far = [(2 * e + c, 2 * (e ^ bits[c][1]) + c) for e, c in cells]
+
+    def swap(value):
+        return lax.ppermute(value, "tensor", [(0, 1), (1, 0)])
+
+    live = jnp.arange(tok_dev, dtype=jnp.int32) < live_count[0]
+    named = jnp.where(live[:, None], route_ids, -1).astype(f32)
+    table = jnp.concatenate([named, route_weight], 1).T
+    blocks = [tokens]
+    blocks.append(lax.ppermute(tokens, BOTH, turn(1)))
+    beside = [lax.ppermute(tokens, BOTH, near)]
+    table = jnp.stack([table, lax.ppermute(table, BOTH, near)])
+    tables = [table] + [lax.ppermute(table, BOTH, turn(k)) for k in range(1, ring)]
+    for _ in range(2, ring):
+        blocks.append(lax.ppermute(blocks[-1], BOTH, turn(1)))
+    for k in range(1, ring):
+        beside.append(lax.ppermute(blocks[k], BOTH, near))
+    far_bit = jnp.where(first, bits[0][1], bits[1][1])
+
+    def picking(table, expert):
+        match = (table[:, :top] == expert.astype(f32)).astype(f32)
+        hit = jnp.sum(match, 1)
+        earlier = jnp.tril(jnp.ones((tok_dev, tok_dev), f32), -1)
+        rank = jnp.sum(hit[:, None, :] * earlier, -1)
+        slot = jnp.arange(capacity, dtype=f32)
+        pick = (rank[:, None, :] == slot[:, None]) & (hit[:, None, :] > 0)
+        weight = jnp.sum(match * table[:, top:], 1)
+        return pick, jnp.where(pick, weight[:, None, :], 0.0)
+
+    gate_w, up_w, down_w = w_gate[0], w_up[0], w_down[0]
+    own_down = lax.dynamic_slice_in_dim(down_w, core * width, width, 1)
+    other_down = lax.dynamic_slice_in_dim(down_w, (1 - core) * width, width, 1)
+
+    size = ring // CHUNKS
+    count = size * capacity
+    mine = [picking(t, me) for t in tables]
+    theirs = [picking(t, me ^ far_bit) for t in tables]
+
+    def select(picks, k, which):
+        matrix = picks[k][0][which].astype(bf16)
+        x = (blocks, beside)[which][k]
+        return jnp.dot(matrix, x, preferred_element_type=f32).astype(bf16)
+
+    got = [
+        lax.ppermute(jnp.concatenate([select(theirs, k, 0), select(theirs, k, 1)], 0), BOTH, far)
+        for k in range(ring)
+    ]
+    partial = []
+    for chunk in range(CHUNKS):
+        ks = slice(chunk * size, (chunk + 1) * size)
+        kept = [jnp.concatenate([select(mine, k, w) for k in range(ring)[ks]], 0) for w in (0, 1)]
+        came = [
+            jnp.concatenate([g[w * capacity : (w + 1) * capacity] for g in got[ks]], 0)
+            for w in (0, 1)
+        ]
+        a, b = jnp.where(first, came[0], kept[1]), jnp.where(first, kept[1], came[0])
+        rows = jnp.concatenate([kept[0], a, b, came[1]], 0)
+        peer = swap(rows)
+        full = jnp.concatenate(
+            [jnp.where(first, rows, peer), jnp.where(first, peer, rows)], 1
+        )
+        gate = jnp.dot(full, gate_w, preferred_element_type=f32)
+        up = jnp.dot(full, up_w, preferred_element_type=f32)
+        hidden = (jax.nn.silu(gate) * up).astype(bf16)
+        there = jnp.dot(hidden, other_down, preferred_element_type=f32).astype(bf16)
+        here = jnp.dot(hidden, own_down, preferred_element_type=f32)
+        out = (here + swap(there).astype(f32)).astype(bf16).reshape(4, count, width)
+        one = jnp.where(first, out[1], out[2])
+        back = lax.ppermute(jnp.concatenate([one, out[3]], 0), BOTH, far)
+        near_own = jnp.where(first, out[2], out[1])
+
+        def spread(which, own, remote):
+            exact = jnp.concatenate(
+                [
+                    block_diagonal(jnp.stack([p[1][which] for p in picks[ks]]))
+                    for picks in (mine, theirs)
+                ],
+                0,
+            )
+            high = exact.astype(bf16)
+            low = (exact - high.astype(f32)).astype(bf16)
+            values = jnp.concatenate([own, remote], 0)
+            return sum(
+                lax.dot_general(
+                    part, values, (((0,), (0,)), ((), ())), preferred_element_type=f32
+                )
+                for part in (high, low)
+            )
+
+        beside_sum = spread(1, near_own, back[count:]).astype(bf16)
+        arrived = jnp.concatenate(
+            [
+                lax.ppermute(beside_sum[k * tok_dev : (k + 1) * tok_dev], BOTH, near)
+                for k in range(size)
+            ],
+            0,
+        )
+        total = spread(0, out[0], back[:count]) + arrived.astype(f32)
+        partial += [total[k * tok_dev : (k + 1) * tok_dev] for k in range(size)]
+
+    running = partial[1]
+    for k in range(2, ring + 1):
+        running = partial[k % ring] + lax.ppermute(running.astype(bf16), BOTH, turn(1)).astype(f32)
+    return running.astype(bf16)[owner_slot]
+
+
 def solution(mesh):
+    groups, cores = mesh.shape["expert"], mesh.shape["tensor"]
+
+    def body(tokens, *rest):
+        tok_dev, top = rest[3].shape
+        capacity = 3 * tok_dev * top // (2 * groups)
+        blocks_pay = cores == 2 and groups % 8 == 0 and tok_dev <= 2 * capacity
+        return (tree_body if blocks_pay else exchange_body)(tokens, *rest)
+
     placed = (
         P("expert", "tensor"),
         P("expert", None, "tensor"),

time: 280 us -> 162 us (0.58)
  the two profiles are of different devices: /device:TPU:14 before, /device:TPU:0 now
where the time goes in v1:
time: 162 us; the launch traced here: 161 us
  waiting for transfers between devices  63.7 us (39%)
  starting transfers between devices  31.5 us (19%)
  matrix products  27.9 us (17%)
  local copies, waits for them, and re-layouts  21.6 us (13%)
  other arithmetic  14.7 us (9%)
    ppermute x3, waiting for transfers between devices, tree_body(): lax.ppermute(running.astype(bf16), BOTH, turn(1)).astype(f32)  20.7 us
    ppermute x2, waiting for transfers between devices, tree_body(): back = lax.ppermute(jnp.concatenate([one, out[3]], 0), BOTH, far)  17 us
    concatenate x2, local copies, waits for them, and re-layouts, tree_body(): rows = jnp.concatenate([kept[0], a, b, came[1]], 0)  10.6 us
    ppermute x3, waiting for transfers between devices, tree_body(): beside.append(lax.ppermute(blocks[k], BOTH, near))  10 us
    dot_general x2, matrix products, tree_body(): gate = jnp.dot(full, gate_w, preferred_element_type=f32)  8.25 us
    ppermute x3, starting transfers between devices, tree_body(): lax.ppermute(table, BOTH, turn(k))  6.41 us
    dot_general x16, matrix products, select(): return jnp.dot(matrix, x, preferred_element_type=f32).astype(bf16)  6.03 us
    another operation x8, other arithmetic, spread(): jnp.stack([p[1][which] for p in picks[ks]])  5.46 us
  transfers between devices with their start and end apart: 28, of which 16 were waited for; matrix products, arithmetic and copies ran while one was open for 31% of the time, Pallas kernels for 0%

profile of v1, /device:TPU:0, one launch (start us, length us, event | category | flops | bytes accessed | tf_op | source)
XLA Modules:
  0.0 160.9 jit_solution(8851160285718234896)
XLA Ops:
  0.0 3.1 %collective-permute-start.2 = (bf16[64,2560]{1,0:T(8,128)(2,1)}, bf16[64,2560]{1,0:T(8,128)(2,1)S(1)}, u32[]{:S(2)}, u32[]{:S(2)}) collective-permute-start(bf16[64,2560]{1,0:T(8,128)(2,1)} %param.8), channel_id=1, source_target_pairs={{0,8},{1,9},{2,10},{3,11},{4,12},{5,13},{6,14},{7,15},{8,16},{9,17... | collective-permute-start | bytes 983048 | tf_op jit(solution)/shard_map/ppermute | solution.py:90
  7.2 3.2 %collective-permute-done = f32[12,64]{1,0:T(8,128)S(1)} collective-permute-done((f32[12,64]{1,0:T(8,128)S(1)}, f32[12,64]{1,0:T(8,128)S(1)}, u32[]{:S(2)}, u32[]{:S(2)}) %collective-permute-start) | collective-permute-done | bytes 3104 | tf_op jit(solution)/shard_map/ppermute | solution.py:92
  10.4 2.6 %collective-permute-start.12 = (f32[2,12,64]{2,1,0:T(8,128)S(1)}, f32[2,12,64]{2,1,0:T(8,128)S(1)}, u32[]{:S(2)}, u32[]{:S(2)}) collective-permute-start(f32[2,12,64]{2,1,0:T(8,128)S(1)} %pad_maximum_fusion.36), channel_id=1, source_target_pairs={{0,16},{1,17},{2,18},{3,19},{4,20},{5,21},{6,22},{7,23},{8,24},{9,... | collective-permute-start | bytes 18440 | tf_op jit(solution)/shard_map/ppermute | solution.py:93
  13.1 3.8 %collective-permute-start.13 = (f32[2,12,64]{2,1,0:T(8,128)S(1)}, f32[2,12,64]{2,1,0:T(8,128)S(1)}, u32[]{:S(2)}, u32[]{:S(2)}) collective-permute-start(f32[2,12,64]{2,1,0:T(8,128)S(1)} %pad_maximum_fusion.36), channel_id=1, source_target_pairs={{0,24},{1,25},{2,26},{3,27},{4,28},{5,29},{6,30},{7,31},{8,0},{9,1... | collective-permute-start | bytes 18440 | tf_op jit(solution)/shard_map/ppermute | solution.py:93
  30.0 5.0 %collective-permute-done.5 = bf16[64,2560]{1,0:T(8,128)(2,1)S(1)} collective-permute-done((bf16[64,2560]{1,0:T(8,128)(2,1)S(1)}, bf16[64,2560]{1,0:T(8,128)(2,1)S(1)}, u32[]{:S(2)}, u32[]{:S(2)}) %collective-permute-start.5) | collective-permute-done | bytes 327712 | tf_op jit(solution)/shard_map/ppermute | solution.py:97
  40.1 4.2 %collective-permute-done.16 = bf16[64,2560]{1,0:T(8,128)(2,1)S(1)} collective-permute-done((bf16[64,2560]{1,0:T(8,128)(2,1)S(1)}, bf16[64,2560]{1,0:T(8,128)(2,1)S(1)}, u32[]{:S(2)}, u32[]{:S(2)}) %collective-permute-start.16) | collective-permute-done | bytes 327712 | tf_op jit(solution)/shard_map/ppermute | solution.py:97
  51.9 3.6 %concatenate.81 = bf16[288,2560]{1,0:T(8,128)(2,1)S(1)} concatenate(bf16[36,2560]{1,0:T(8,128)(2,1)S(1)} %convolution_convert_fusion.17, bf16[36,2560]{1,0:T(8,128)(2,1)S(1)} %convolution_convert_fusion.16, bf16[72,2560]{1,0:T(8,128)(2,1)S(1)} %get-tuple-element.44, bf16[72,2560]{1,0:T(8,128)(2,1)S(1)} %get-tuple-element.43, bf16[36,2560]{1,0:T(8,128)(2,1)} %get-tuple-element.59, ...), dimensions={0} | concatenate | bytes 2949120 | tf_op jit(solution)/shard_map/concatenate | solution.py:137
  59.9 1.8 %fusion.79 = (bf16[36,2560]{1,0:T(8,128)(2,1)}, bf16[36,2560]{1,0:T(8,128)(2,1)S(1)}) fusion(bf16[72,2560]{1,0:T(8,128)(2,1)} %collective-permute-done.17), kind=kLoop, calls=%fused_computation.243 | loop fusion | bytes 737280 | tf_op jit(solution)/shard_map/slice | solution.py:133
  61.7 4.5 %collective-permute-done.19 = bf16[72,2560]{1,0:T(8,128)(2,1)S(1)} collective-permute-done((bf16[72,2560]{1,0:T(8,128)(2,1)S(1)}, bf16[72,2560]{1,0:T(8,128)(2,1)S(1)}, u32[]{:S(2)}, u32[]{:S(2)}) %collective-permute-start.19) | collective-permute-done | bytes 368672 | tf_op jit(solution)/shard_map/ppermute | solution.py:125
  67.8 7.1 %concatenate.93 = bf16[288,2560]{1,0:T(8,128)(2,1)S(1)} concatenate(bf16[36,2560]{1,0:T(8,128)(2,1)S(1)} %convolution_convert_fusion.9, bf16[36,2560]{1,0:T(8,128)(2,1)} %convolution_convert_fusion.8, bf16[72,2560]{1,0:T(8,128)(2,1)} %get-tuple-element.42, bf16[72,2560]{1,0:T(8,128)(2,1)S(1)} %get-tuple-element.41, bf16[36,2560]{1,0:T(8,128)(2,1)} %get-tuple-element.55, ...), dimensions={0} | concatenate | bytes 2949120 | tf_op jit(solution)/shard_map/concatenate | solution.py:137
  81.4 2.4 %broadcast_select_fusion.1 = (bf16[288,2560]{1,0:T(8,128)(2,1)S(1)}, bf16[288,2560]{1,0:T(8,128)(2,1)S(1)}, bf16[288,2560]{1,0:T(8,128)(2,1)S(1)}, bf16[288,2560]{1,0:T(8,128)(2,1)S(1)}) fusion(bf16[288,2560]{1,0:T(8,128)(2,1)S(1)} %concatenate.93, bf16[288,2560]{1,0:T(8,128)(2,1)} %collective-permute-done.20, pred[]{:T(512)S(6)} %eq.181, ...), kind=kLoop, calls=%fused_computation.50 | loop fusion | flops 2949120 | bytes 11796481 | tf_op jit(solution)/shard_map/jit(_where)/select_n | solution.py:140
  83.8 5.8 %fusion.6 = f32[288,768]{1,0:T(8,128)S(1)} fusion(bf16[1,5120,768]{2,1,0:T(8,128)(2,1)} %param.9, bf16[288,2560]{1,0:T(8,128)(2,1)S(1)} %get-tuple-element.95, bf16[288,2560]{1,0:T(8,128)(2,1)S(1)} %get-tuple-element.96), kind=kOutput, calls=%fused_computation.7 | convolution fusion | flops 2270822400 | bytes 11698176 | tf_op jit(solution)/shard_map/dot_general | solution.py:142
  89.7 2.5 %multiply_convert_fusion.1 = bf16[288,768]{1,0:T(8,128)(2,1)S(1)} fusion(f32[288,768]{1,0:T(8,128)S(1)} %fusion.6, bf16[1,5120,768]{2,1,0:T(8,128)(2,1)S(1)} %bitcast.110, bf16[288,2560]{1,0:T(8,128)(2,1)S(1)} %get-tuple-element.95, bf16[288,2560]{1,0:T(8,128)(2,1)S(1)} %get-tuple-element.96), kind=kOutput, calls=%fused_computation.54 | convolution fusion | flops 2272149504 | bytes 12140544 | tf_op jit(solution)/shard_map/dot_general | solution.py:143
  94.1 2.4 %fusion.4 = f32[288,768]{1,0:T(8,128)S(1)} fusion(bf16[1,5120,768]{2,1,0:T(8,128)(2,1)S(1)} %bitcast.108, bf16[288,2560]{1,0:T(8,128)(2,1)S(1)} %get-tuple-element.30, bf16[288,2560]{1,0:T(8,128)(2,1)S(1)} %get-tuple-element.29), kind=kOutput, calls=%fused_computation.5 | convolution fusion | flops 2270822400 | bytes 11698176 | tf_op jit(solution)/shard_map/dot_general | solution.py:142
  96.5 2.5 %multiply_convert_fusion = bf16[288,768]{1,0:T(8,128)(2,1)S(1)} fusion(f32[288,768]{1,0:T(8,128)S(1)} %fusion.4, bf16[1,5120,768]{2,1,0:T(8,128)(2,1)S(1)} %bitcast.110, bf16[288,2560]{1,0:T(8,128)(2,1)S(1)} %get-tuple-element.30, bf16[288,2560]{1,0:T(8,128)(2,1)S(1)} %get-tuple-element.29), kind=kOutput, calls=%fused_computation.53 | convolution fusion | flops 2272149504 | bytes 12140544 | tf_op jit(solution)/shard_map/dot_general | solution.py:143
  100.5 1.6 add_convert_fusion.1
  106.4 7.4 %collective-permute-done.9 = bf16[144,2560]{1,0:T(8,128)(2,1)S(1)} collective-permute-done((bf16[144,2560]{1,0:T(8,128)(2,1)S(1)}, bf16[144,2560]{1,0:T(8,128)(2,1)S(1)}, u32[]{:S(2)}, u32[]{:S(2)}) %collective-permute-start.9) | collective-permute-done | bytes 737312 | tf_op jit(solution)/shard_map/ppermute | solution.py:149
  116.7 9.6 %collective-permute-done.22 = bf16[144,2560]{1,0:T(8,128)(2,1)S(1)} collective-permute-done((bf16[144,2560]{1,0:T(8,128)(2,1)S(1)}, bf16[144,2560]{1,0:T(8,128)(2,1)S(1)}, u32[]{:S(2)}, u32[]{:S(2)}) %collective-permute-start.22) | collective-permute-done | bytes 737312 | tf_op jit(solution)/shard_map/ppermute | solution.py:149
  130.1 1.9 %collective-permute-start.25 = (bf16[64,2560]{1,0:T(8,128)(2,1)S(1)}, bf16[64,2560]{1,0:T(8,128)(2,1)S(1)}, u32[]{:S(2)}, u32[]{:S(2)}) collective-permute-start(bf16[64,2560]{1,0:T(8,128)(2,1)S(1)} %slice.455), channel_id=1, source_target_pairs={{0,8},{1,9},{2,10},{3,11},{4,12},{5,13},{6,14},{7,15},{8,16},{9,17... | collective-permute-start | bytes 983048 | tf_op jit(solution)/shard_map/ppermute | solution.py:183
  132.4 1.9 %collective-permute-done.24 = bf16[64,2560]{1,0:T(8,128)(2,1)S(1)} collective-permute-done((bf16[64,2560]{1,0:T(8,128)(2,1)S(1)}, bf16[64,2560]{1,0:T(8,128)(2,1)S(1)}, u32[]{:S(2)}, u32[]{:S(2)}) %collective-permute-start.24) | collective-permute-done | bytes 327712 | tf_op jit(solution)/shard_map/ppermute | solution.py:173
  134.3 3.5 %collective-permute-done.23 = bf16[64,2560]{1,0:T(8,128)(2,1)S(1)} collective-permute-done((bf16[64,2560]{1,0:T(8,128)(2,1)S(1)}, bf16[64,2560]{1,0:T(8,128)(2,1)S(1)}, u32[]{:S(2)}, u32[]{:S(2)}) %collective-permute-start.23) | collective-permute-done | bytes 327712 | tf_op jit(solution)/shard_map/ppermute | solution.py:173
  138.2 2.4 %collective-permute-done.25 = bf16[64,2560]{1,0:T(8,128)(2,1)S(1)} collective-permute-done((bf16[64,2560]{1,0:T(8,128)(2,1)S(1)}, bf16[64,2560]{1,0:T(8,128)(2,1)S(1)}, u32[]{:S(2)}, u32[]{:S(2)}) %collective-permute-start.25) | collective-permute-done | bytes 327712 | tf_op jit(solution)/shard_map/ppermute | solution.py:183
  140.7 9.6 %collective-permute-done.26 = bf16[64,2560]{1,0:T(8,128)(2,1)S(1)} collective-permute-done((bf16[64,2560]{1,0:T(8,128)(2,1)S(1)}, bf16[64,2560]{1,0:T(8,128)(2,1)S(1)}, u32[]{:S(2)}, u32[]{:S(2)}) %collective-permute-start.26) | collective-permute-done | bytes 327712 | tf_op jit(solution)/shard_map/ppermute | solution.py:183
  150.5 8.8 %collective-permute-done.27 = bf16[64,2560]{1,0:T(8,128)(2,1)S(1)} collective-permute-done((bf16[64,2560]{1,0:T(8,128)(2,1)S(1)}, bf16[64,2560]{1,0:T(8,128)(2,1)S(1)}, u32[]{:S(2)}, u32[]{:S(2)}) %collective-permute-start.27) | collective-permute-done | bytes 327712 | tf_op jit(solution)/shard_map/ppermute | solution.py:183
  (182 shorter events, 58.6 us)
Async XLA Ops:
  0.0 27.9 %collective-permute-start.2 = (bf16[64,2560]{1,0:T(8,128)(2,1)}, bf16[64,2560]{1,0:T(8,128)(2,1)S(1)}, u32[]{:S(2)}, u32[]{:S(2)}) collective-permute-start(bf16[64,2560]{1,0:T(8,128)(2,1)} %param.8), channel_id=1, source_target_pairs={{0,8},{1,9},{2,10},{3,11},{4,12},{5,13},{6,14},{7,15},{8,16},{9,17... | collective-permute-start | bytes 983048 | tf_op jit(solution)/shard_map/ppermute | solution.py:90
  3.1 23.0 %collective-permute-start.3 = (bf16[64,2560]{1,0:T(8,128)(2,1)}, bf16[64,2560]{1,0:T(8,128)(2,1)S(1)}, u32[]{:S(2)}, u32[]{:S(2)}) collective-permute-start(bf16[64,2560]{1,0:T(8,128)(2,1)} %param.8), channel_id=1, source_target_pairs={{0,4},{1,3},{2,6},{3,1},{4,0},{5,7},{6,2},{7,5},{8,12},{9,11},{10,... | collective-permute-start | bytes 983048 | tf_op jit(solution)/shard_map/ppermute | solution.py:91
  10.4 6.5 %collective-permute-start.12 = (f32[2,12,64]{2,1,0:T(8,128)S(1)}, f32[2,12,64]{2,1,0:T(8,128)S(1)}, u32[]{:S(2)}, u32[]{:S(2)}) collective-permute-start(f32[2,12,64]{2,1,0:T(8,128)S(1)} %pad_maximum_fusion.36), channel_id=1, source_target_pairs={{0,16},{1,17},{2,18},{3,19},{4,20},{5,21},{6,22},{7,23},{8,24},{9,... | collective-permute-start | bytes 18440 | tf_op jit(solution)/shard_map/ppermute | solution.py:93
  26.4 13.0 %collective-permute-start.4 = (bf16[72,2560]{1,0:T(8,128)(2,1)S(1)}, bf16[72,2560]{1,0:T(8,128)(2,1)S(1)}, u32[]{:S(2)}, u32[]{:S(2)}) collective-permute-start(bf16[72,2560]{1,0:T(8,128)(2,1)S(1)} %pad_maximum_fusion.20), channel_id=1, source_target_pairs={{0,2},{1,5},{2,0},{3,7},{4,6},{5,1},{6,4},{7,3},{8,10},{9,13},{10,... | collective-permute-start | bytes 1105928 | tf_op jit(solution)/shard_map/ppermute | solution.py:125
  27.9 9.0 %collective-permute-start.14 = (bf16[64,2560]{1,0:T(8,128)(2,1)S(1)}, bf16[64,2560]{1,0:T(8,128)(2,1)S(1)}, u32[]{:S(2)}, u32[]{:S(2)}) collective-permute-start(bf16[64,2560]{1,0:T(8,128)(2,1)S(1)} %collective-permute-done.2), channel_id=1, source_target_pairs={{0,8},{1,9},{2,10},{3,11},{4,12},{5,13},{6,14},{7,15},{8,16},{9,17... | collective-permute-start | bytes 983048 | tf_op jit(solution)/shard_map/ppermute | solution.py:95
  27.9 7.1 %collective-permute-start.5 = (bf16[64,2560]{1,0:T(8,128)(2,1)S(1)}, bf16[64,2560]{1,0:T(8,128)(2,1)S(1)}, u32[]{:S(2)}, u32[]{:S(2)}) collective-permute-start(bf16[64,2560]{1,0:T(8,128)(2,1)S(1)} %collective-permute-done.2), channel_id=1, source_target_pairs={{0,4},{1,3},{2,6},{3,1},{4,0},{5,7},{6,2},{7,5},{8,12},{9,11},{10,... | collective-permute-start | bytes 983048 | tf_op jit(solution)/shard_map/ppermute | solution.py:97
  35.3 15.7 %collective-permute-start.6 = (bf16[72,2560]{1,0:T(8,128)(2,1)S(1)}, bf16[72,2560]{1,0:T(8,128)(2,1)S(1)}, u32[]{:S(2)}, u32[]{:S(2)}) collective-permute-start(bf16[72,2560]{1,0:T(8,128)(2,1)S(1)} %pad_maximum_fusion.21), channel_id=1, source_target_pairs={{0,2},{1,5},{2,0},{3,7},{4,6},{5,1},{6,4},{7,3},{8,10},{9,13},{10,... | collective-permute-start | bytes 1105928 | tf_op jit(solution)/shard_map/ppermute | solution.py:125
  36.9 10.8 %collective-permute-start.15 = (bf16[64,2560]{1,0:T(8,128)(2,1)S(1)}, bf16[64,2560]{1,0:T(8,128)(2,1)S(1)}, u32[]{:S(2)}, u32[]{:S(2)}) collective-permute-start(bf16[64,2560]{1,0:T(8,128)(2,1)S(1)} %collective-permute-done.14), channel_id=1, source_target_pairs={{0,8},{1,9},{2,10},{3,11},{4,12},{5,13},{6,14},{7,15},{8,16},{9,17... | collective-permute-start | bytes 983048 | tf_op jit(solution)/shard_map/ppermute | solution.py:95
  37.3 7.1 %collective-permute-start.16 = (bf16[64,2560]{1,0:T(8,128)(2,1)S(1)}, bf16[64,2560]{1,0:T(8,128)(2,1)S(1)}, u32[]{:S(2)}, u32[]{:S(2)}) collective-permute-start(bf16[64,2560]{1,0:T(8,128)(2,1)S(1)} %collective-permute-done.14), channel_id=1, source_target_pairs={{0,4},{1,3},{2,6},{3,1},{4,0},{5,7},{6,2},{7,5},{8,12},{9,11},{10,... | collective-permute-start | bytes 983048 | tf_op jit(solution)/shard_map/ppermute | solution.py:97
  45.4 14.6 %collective-permute-start.17 = (bf16[72,2560]{1,0:T(8,128)(2,1)}, bf16[72,2560]{1,0:T(8,128)(2,1)}, u32[]{:S(2)}, u32[]{:S(2)}) collective-permute-start(bf16[72,2560]{1,0:T(8,128)(2,1)} %pad_maximum_fusion.24), channel_id=1, source_target_pairs={{0,2},{1,5},{2,0},{3,7},{4,6},{5,1},{6,4},{7,3},{8,10},{9,13},{10,... | collective-permute-start | bytes 1105928 | tf_op jit(solution)/shard_map/ppermute | solution.py:125
  47.7 9.6 %collective-permute-start.18 = (bf16[64,2560]{1,0:T(8,128)(2,1)S(1)}, bf16[64,2560]{1,0:T(8,128)(2,1)S(1)}, u32[]{:S(2)}, u32[]{:S(2)}) collective-permute-start(bf16[64,2560]{1,0:T(8,128)(2,1)S(1)} %collective-permute-done.15), channel_id=1, source_target_pairs={{0,4},{1,3},{2,6},{3,1},{4,0},{5,7},{6,2},{7,5},{8,12},{9,11},{10,... | collective-permute-start | bytes 983048 | tf_op jit(solution)/shard_map/ppermute | solution.py:97
  55.5 25.9 %collective-permute-start.7 = (bf16[288,2560]{1,0:T(8,128)(2,1)S(1)}, bf16[288,2560]{1,0:T(8,128)(2,1)}, u32[]{:S(2)}, u32[]{:S(2)}) collective-permute-start(bf16[288,2560]{1,0:T(8,128)(2,1)S(1)} %concatenate.81), channel_id=1, source_target_pairs={{0,1},{1,0},{2,3},{3,2},{4,5},{5,4},{6,7},{7,6},{8,9},{9,8},{10,11... | collective-permute-start | bytes 4423688 | tf_op jit(solution)/shard_map/ppermute | solution.py:84
  58.6 7.6 %collective-permute-start.19 = (bf16[72,2560]{1,0:T(8,128)(2,1)S(1)}, bf16[72,2560]{1,0:T(8,128)(2,1)S(1)}, u32[]{:S(2)}, u32[]{:S(2)}) collective-permute-start(bf16[72,2560]{1,0:T(8,128)(2,1)S(1)} %pad_maximum_fusion.25), channel_id=1, source_target_pairs={{0,2},{1,5},{2,0},{3,7},{4,6},{5,1},{6,4},{7,3},{8,10},{9,13},{10,... | collective-permute-start | bytes 1105928 | tf_op jit(solution)/shard_map/ppermute | solution.py:125
  74.9 6.5 %collective-permute-start.20 = (bf16[288,2560]{1,0:T(8,128)(2,1)S(1)}, bf16[288,2560]{1,0:T(8,128)(2,1)}, u32[]{:S(2)}, u32[]{:S(2)}) collective-permute-start(bf16[288,2560]{1,0:T(8,128)(2,1)S(1)} %concatenate.93), channel_id=1, source_target_pairs={{0,1},{1,0},{2,3},{3,2},{4,5},{5,4},{6,7},{7,6},{8,9},{9,8},{10,11... | collective-permute-start | bytes 4423688 | tf_op jit(solution)/shard_map/ppermute | solution.py:84
  93.6 6.9 %collective-permute-start.8 = (bf16[288,2560]{1,0:T(8,128)(2,1)S(1)}, bf16[288,2560]{1,0:T(8,128)(2,1)S(1)}, u32[]{:S(2)}, u32[]{:S(2)}) collective-permute-start(bf16[288,2560]{1,0:T(8,128)(2,1)S(1)} %convolution_convert_fusion.1), channel_id=1, source_target_pairs={{0,1},{1,0},{2,3},{3,2},{4,5},{5,4},{6,7},{7,6},{8,9},{9,8},{10,11... | collective-permute-start | bytes 4423688 | tf_op jit(solution)/shard_map/ppermute | solution.py:84
  102.2 11.5 %collective-permute-start.9 = (bf16[144,2560]{1,0:T(8,128)(2,1)S(1)}, bf16[144,2560]{1,0:T(8,128)(2,1)S(1)}, u32[]{:S(2)}, u32[]{:S(2)}) collective-permute-start(bf16[144,2560]{1,0:T(8,128)(2,1)S(1)} %pad_maximum_fusion.6), channel_id=1, source_target_pairs={{0,2},{1,5},{2,0},{3,7},{4,6},{5,1},{6,4},{7,3},{8,10},{9,13},{10,... | collective-permute-start | bytes 2211848 | tf_op jit(solution)/shard_map/ppermute | solution.py:149
  105.2 21.1 %collective-permute-start.22 = (bf16[144,2560]{1,0:T(8,128)(2,1)S(1)}, bf16[144,2560]{1,0:T(8,128)(2,1)S(1)}, u32[]{:S(2)}, u32[]{:S(2)}) collective-permute-start(bf16[144,2560]{1,0:T(8,128)(2,1)S(1)} %pad_maximum_fusion.9), channel_id=1, source_target_pairs={{0,2},{1,5},{2,0},{3,7},{4,6},{5,1},{6,4},{7,3},{8,10},{9,13},{10,... | collective-permute-start | bytes 2211848 | tf_op jit(solution)/shard_map/ppermute | solution.py:149
  114.6 15.1 %collective-permute-start.11 = (bf16[64,2560]{1,0:T(8,128)(2,1)S(1)}, bf16[64,2560]{1,0:T(8,128)(2,1)S(1)}, u32[]{:S(2)}, u32[]{:S(2)}) collective-permute-start(bf16[64,2560]{1,0:T(8,128)(2,1)S(1)} %get-tuple-element.52), channel_id=1, source_target_pairs={{0,4},{1,3},{2,6},{3,1},{4,0},{5,7},{6,2},{7,5},{8,12},{9,11},{10,... | collective-permute-start | bytes 983048 | tf_op jit(solution)/shard_map/ppermute | solution.py:173
  115.6 14.1 %collective-permute-start.10 = (bf16[64,2560]{1,0:T(8,128)(2,1)S(1)}, bf16[64,2560]{1,0:T(8,128)(2,1)S(1)}, u32[]{:S(2)}, u32[]{:S(2)}) collective-permute-start(bf16[64,2560]{1,0:T(8,128)(2,1)S(1)} %get-tuple-element.51), channel_id=1, source_target_pairs={{0,4},{1,3},{2,6},{3,1},{4,0},{5,7},{6,2},{7,5},{8,12},{9,11},{10,... | collective-permute-start | bytes 983048 | tf_op jit(solution)/shard_map/ppermute | solution.py:173
  127.2 7.1 %collective-permute-start.24 = (bf16[64,2560]{1,0:T(8,128)(2,1)S(1)}, bf16[64,2560]{1,0:T(8,128)(2,1)S(1)}, u32[]{:S(2)}, u32[]{:S(2)}) collective-permute-start(bf16[64,2560]{1,0:T(8,128)(2,1)S(1)} %get-tuple-element.50), channel_id=1, source_target_pairs={{0,4},{1,3},{2,6},{3,1},{4,0},{5,7},{6,2},{7,5},{8,12},{9,11},{10,... | collective-permute-start | bytes 983048 | tf_op jit(solution)/shard_map/ppermute | solution.py:173
  128.1 9.8 %collective-permute-start.23 = (bf16[64,2560]{1,0:T(8,128)(2,1)S(1)}, bf16[64,2560]{1,0:T(8,128)(2,1)S(1)}, u32[]{:S(2)}, u32[]{:S(2)}) collective-permute-start(bf16[64,2560]{1,0:T(8,128)(2,1)S(1)} %get-tuple-element.49), channel_id=1, source_target_pairs={{0,4},{1,3},{2,6},{3,1},{4,0},{5,7},{6,2},{7,5},{8,12},{9,11},{10,... | collective-permute-start | bytes 983048 | tf_op jit(solution)/shard_map/ppermute | solution.py:173
  130.1 10.5 %collective-permute-start.25 = (bf16[64,2560]{1,0:T(8,128)(2,1)S(1)}, bf16[64,2560]{1,0:T(8,128)(2,1)S(1)}, u32[]{:S(2)}, u32[]{:S(2)}) collective-permute-start(bf16[64,2560]{1,0:T(8,128)(2,1)S(1)} %slice.455), channel_id=1, source_target_pairs={{0,8},{1,9},{2,10},{3,11},{4,12},{5,13},{6,14},{7,15},{8,16},{9,17... | collective-permute-start | bytes 983048 | tf_op jit(solution)/shard_map/ppermute | solution.py:183
  140.7 9.6 %collective-permute-start.26 = (bf16[64,2560]{1,0:T(8,128)(2,1)S(1)}, bf16[64,2560]{1,0:T(8,128)(2,1)S(1)}, u32[]{:S(2)}, u32[]{:S(2)}) collective-permute-start(bf16[64,2560]{1,0:T(8,128)(2,1)S(1)} %fusion.22), channel_id=1, source_target_pairs={{0,8},{1,9},{2,10},{3,11},{4,12},{5,13},{6,14},{7,15},{8,16},{9,17... | collective-permute-start | bytes 983048 | tf_op jit(solution)/shard_map/ppermute | solution.py:183
  150.4 8.9 %collective-permute-start.27 = (bf16[64,2560]{1,0:T(8,128)(2,1)S(1)}, bf16[64,2560]{1,0:T(8,128)(2,1)S(1)}, u32[]{:S(2)}, u32[]{:S(2)}) collective-permute-start(bf16[64,2560]{1,0:T(8,128)(2,1)S(1)} %fusion.23), channel_id=1, source_target_pairs={{0,8},{1,9},{2,10},{3,11},{4,12},{5,13},{6,14},{7,15},{8,16},{9,17... | collective-permute-start | bytes 983048 | tf_op jit(solution)/shard_map/ppermute | solution.py:183
  (13 other events, 105.1 us)

commit v2 on v0

--- a/solution.py
+++ b/solution.py
@@ -1,10 +1,18 @@
+import functools
+
 import jax
 import jax.numpy as jnp
+import numpy as np
 from jax import lax
+from jax.experimental import pallas as pl
+from jax.experimental.pallas import tpu as pltpu
 from jax.sharding import PartitionSpec as P
 
-
-def body(tokens, w_gate, w_up, w_down, route_ids, route_weight, live_count, owner_slot):
+BF16, F32 = jnp.bfloat16, jnp.float32
+BOTH = ("expert", "tensor")
+
+
+def exchange_body(tokens, w_gate, w_up, w_down, route_ids, route_weight, live_count, owner_slot):
     tok_dev, top = route_ids.shape
     groups = lax.axis_size("expert")
     capacity = 3 * tok_dev * top // (2 * groups)
@@ -51,7 +59,258 @@
     return mixed.astype(jnp.bfloat16)
 
 
+def call(kernel, outs, scalars, operands, grid, in_specs, out_specs, scratch=(), flops=0):
+    moved = sum(x.size * x.dtype.itemsize for x in operands)
+    return pl.pallas_call(
+        kernel,
+        out_shape=outs,
+        grid_spec=pltpu.PrefetchScalarGridSpec(
+            num_scalar_prefetch=1,
+            grid=grid,
+            in_specs=in_specs,
+            out_specs=out_specs,
+            scratch_shapes=scratch,
+        ),
+        compiler_params=pltpu.CompilerParams(vmem_limit_bytes=2**22),
+        cost_estimate=pl.CostEstimate(flops=flops, bytes_accessed=moved, transcendentals=0),
+    )(scalars, *operands)
+
+
+def whole(x):
+    return pl.BlockSpec(x.shape, lambda i, s: (0,) * len(x.shape))
+
+
+def iota(shape, dim):
+    return lax.broadcasted_iota(jnp.int32, shape, dim)
+
+
+def targets(table, expert, top, capacity):
+    lanes = table.shape[1]
+    match = table[:top].astype(jnp.int32) == expert
+    hit = jnp.sum(match.astype(F32), 0, keepdims=True)
+    weight = jnp.sum(jnp.where(match, table[8 : 8 + top], 0.0), 0, keepdims=True)
+    row, col = iota((lanes, lanes), 0), iota((lanes, lanes), 1)
+    half = lanes // 2
+    earlier = (row < col) & ((row >= half) == (col >= half))
+    rank = jnp.dot(
+        jnp.broadcast_to(hit, (8, lanes)).astype(BF16),
+        earlier.astype(F32).astype(BF16),
+        preferred_element_type=F32,
+    )[:1]
+    second = (iota((1, lanes), 1) >= half).astype(jnp.int32)
+    slot = rank.astype(jnp.int32) + capacity * second
+    return jnp.where(hit > 0, slot, -1), weight
+
+
+def routing_kernel(top, capacity, s_ref, table_ref, send_ref, keep_ref, high_ref, low_ref):
+    table = table_ref[...]
+    lanes = table.shape[1]
+    half, count = lanes // 2, 2 * capacity
+    depth = -(-2 * count // 128) * 128
+    exact = jnp.zeros((depth, lanes), F32)
+    for which, out_ref in ((0, keep_ref), (1, send_ref)):
+        slot, weight = targets(table, s_ref[which], top, capacity)
+        out_ref[...] = (iota((count, lanes), 0) == slot).astype(F32).astype(BF16)
+        slot = jnp.where(slot >= 0, slot + which * count, -1)
+        exact += jnp.where(iota((depth, lanes), 0) == slot, weight, 0.0)
+    owner = table[top : top + 1].astype(jnp.int32)
+    owner = owner + half * (iota((1, lanes), 1) >= half).astype(jnp.int32)
+    place = (iota((lanes, lanes), 0) == owner).astype(F32).T.astype(BF16)
+    exact = exact.T
+    high = exact.astype(BF16)
+    low = (exact - high.astype(F32)).astype(BF16)
+    for part, out_ref in ((high, high_ref), (low, low_ref)):
+        out_ref[...] = jnp.dot(place, part, preferred_element_type=F32).astype(BF16)
+
+
+def routing(scalars, top, capacity, table):
+    lanes = table.shape[1]
+    depth = -(-4 * capacity // 128) * 128
+    outs = [jax.ShapeDtypeStruct((2 * capacity, lanes), BF16)] * 2
+    outs += [jax.ShapeDtypeStruct((lanes, depth), BF16)] * 2
+    return call(
+        functools.partial(routing_kernel, top, capacity),
+        outs,
+        scalars,
+        [table],
+        (1,),
+        [whole(table)],
+        [whole(x) for x in outs],
+        flops=2**22,
+    )
+
+
+def crossing(capacity, size):
+    count = 2 * capacity
+    source = np.arange(2 * count * size)
+    for p in range(size):
+        kept, came = p * count + capacity, (size + p) * count
+        source[kept : kept + capacity] = np.arange(came, came + capacity)
+        source[came : came + capacity] = np.arange(kept, kept + capacity)
+    return jnp.asarray(source[:, None] == np.arange(2 * count * size)[None, :], BF16)
+
+
+def dot(a, b, kind=F32):
+    return jnp.dot(a, b, preferred_element_type=F32).astype(kind)
+
+
+def tree_body(tokens, w_gate, w_up, w_down, route_ids, route_weight, live_count, owner_slot):
+    tok_dev, top = route_ids.shape
+    width = tokens.shape[1]
+    groups = lax.axis_size("expert")
+    ring = groups // 4
+    capacity = 3 * tok_dev * top // (2 * groups)
+    count = 2 * capacity
+    me = lax.axis_index("expert")
+    core = lax.axis_index("tensor")
+
+    bits = ((2, 1), (1, 2))
+    cells = [(e, c) for e in range(groups) for c in range(2)]
+
+    def turn(places):
+        return [(2 * e + c, 2 * ((e + 4 * places) % groups) + c) for e, c in cells]
+
+    near = [(2 * e + c, 2 * (e ^ bits[c][0]) + c) for e, c in cells]
+    far = [(2 * e + c, 2 * (e ^ bits[c][1]) + c) for e, c in cells]
+    scalars = jnp.stack([me, me ^ jnp.where(core == 0, bits[0][1], bits[1][1]), core])
+
+    def send(name, value, pairs):
+        with jax.named_scope(name):
+            return lax.ppermute(value, BOTH, pairs)
+
+    def swap(value):
+        return lax.ppermute(value, "tensor", [(0, 1), (1, 0)])
+
+    def after(value, *events):
+        return lax.optimization_barrier((value, *events))[0]
+
+    live = jnp.arange(tok_dev, dtype=jnp.int32) < live_count[0]
+    table = jnp.concatenate(
+        [
+            jnp.where(live[:, None], route_ids, -1).astype(F32),
+            owner_slot.astype(F32)[:, None],
+            jnp.zeros((tok_dev, 7 - top), F32),
+            route_weight,
+            jnp.zeros((tok_dev, 8 - top), F32),
+        ],
+        1,
+    ).T
+    def halves(w, dim):
+        return [lax.dynamic_slice_in_dim(w[0], c * width, width, dim) for c in (core, 1 - core)]
+
+    gates, ups, downs = halves(w_gate, 0), halves(w_up, 0), halves(w_down, 1)
+    blocks, tables, beside, made, sent, got = {}, {}, {}, {}, {}, {}
+    arriving, state, back, partial, own_sum, near_sum = {}, {}, {}, {}, {}, {}
+    last = []
+
+    def then(value):
+        return after(value, *last)
+
+    def done(value):
+        last[:] = [value]
+        return value
+
+    def pick(matrix, k):
+        a, b = matrix[:, :tok_dev], matrix[:, tok_dev:]
+        return (dot(a, blocks[k]) + dot(b, beside[k])).astype(BF16)
+
+    def spread(k):
+        blocks[k] = done(then(arriving[k])) if k else tokens
+        if k + 1 < ring:
+            arriving[k + 1] = send(f"ring{k + 1}", blocks[k], turn(1))
+        beside[k] = send(f"near{k}", blocks[k], near)
+        if k:
+            tables[k] = after(tables[k], blocks[k])
+        else:
+            tables[0] = jnp.concatenate([table, send("tnear", table, near)], 1)
+        if k + 1 < ring:
+            tables[k + 1] = send(f"turn{k + 1}", tables[k], turn(1))
+
+    def route(k):
+        made[k] = routing(scalars, top, capacity, then(tables[k]))
+        done(made[k][0])
+
+    def select(k):
+        beside[k] = then(beside[k])
+        sent[k] = done(pick(made[k][0], k))
+        got[k] = send(f"far{k}", sent[k], far)
+
+    def rows(ks):
+        cross = crossing(capacity, len(ks))
+        mine = jnp.concatenate([pick(made[k][1], k) for k in ks] + [then(got[k]) for k in ks])
+        state[ks[0]] = [mine, swap(done(dot(cross, mine, BF16))), cross]
+
+    def own_half(ks):
+        mine = then(state[ks[0]][0])
+        state[ks[0]][0] = done(lax.optimization_barrier((dot(mine, gates[0]), dot(mine, ups[0]))))
+
+    def peer_half(ks):
+        (gate, up), peer, cross = state[ks[0]]
+        peer = then(peer)
+        gate += dot(peer, gates[1])
+        up += dot(peer, ups[1])
+        hidden = after((gate / (1.0 + jnp.exp(-gate)) * up).astype(BF16))
+        crossed = after(dot(cross, hidden, BF16))
+        state[ks[0]] = [hidden, swap(done(dot(crossed, downs[1], BF16)))]
+
+    def finish(ks):
+        hidden, there = state[ks[0]]
+        here = dot(hidden, downs[0])
+        out = (here + then(there).astype(F32)).astype(BF16)
+        came = [out[(len(ks) + p) * count : (len(ks) + p + 1) * count] for p in range(len(ks))]
+        came = done(lax.optimization_barrier(tuple(came)))
+        for p, k in enumerate(ks):
+            back[k] = out[p * count : (p + 1) * count], send(f"back{k}", came[p], far)
+
+    def merge(k):
+        high, low = made[k][2:]
+        stay, came = back[k]
+        came = then(came)
+
+        def add(matrix):
+            return dot(matrix[:, :count], stay) + dot(matrix[:, count : 2 * count], came)
+
+        total = done((add(high[tok_dev:]) + add(low[tok_dev:])).astype(BF16))
+        near_sum[k] = send(f"sum{k}", total, near)
+        own_sum[k] = add(high[:tok_dev]) + add(low[:tok_dev])
+
+    def pass_on(k):
+        total = own_sum[k % ring] + then(near_sum[k % ring]).astype(F32)
+        if k > 1:
+            total += partial[k - 1].astype(F32)
+        total = done(total.astype(BF16))
+        partial[k] = send(f"add{k + 1}", total, turn(1)) if k < ring else total
+
+    passes = {k: [k] for k in range(1, ring - 1)}
+    passes[ring - 1] = [ring - 1, 0]
+    plan = [(spread, 0), (route, 0), (spread, 1), (select, 0), (route, 1), (select, 1), (spread, 2)]
+    for k, ks in passes.items():
+        plan += [(rows, ks), (own_half, ks)]
+        if k + 1 < ring:
+            plan += [(route, k + 1), (select, k + 1)]
+        if k > 2:
+            plan += [(pass_on, k - 2)]
+        plan += [(peer_half, ks)]
+        if k + 2 < ring:
+            plan += [(spread, k + 2)]
+        if k > 1:
+            plan += [(merge, k - 1)]
+        plan += [(finish, ks)]
+    plan += [(pass_on, ring - 2), (merge, ring - 1), (pass_on, ring - 1), (merge, 0)]
+    for stage, which in plan + [(pass_on, ring)]:
+        stage(which)
+    return partial[ring]
+
+
 def solution(mesh):
+    groups, cores = mesh.shape["expert"], mesh.shape["tensor"]
+
+    def body(tokens, *rest):
+        tok_dev, top = rest[3].shape
+        capacity = 3 * tok_dev * top // (2 * groups)
+        blocks_pay = cores == 2 and groups % 8 == 0 and tok_dev <= 2 * capacity
+        return (tree_body if blocks_pay else exchange_body)(tokens, *rest)
+
     placed = (
         P("expert", "tensor"),
         P("expert", None, "tensor"),

time: 280 us -> 108 us (0.39)
  the two profiles are of different devices: /device:TPU:14 before, /device:TPU:0 now
where the time goes in v2:
time: 108 us
  matrix products  37.1 us (34%)
  starting transfers between devices  32.4 us (30%)
  waiting for transfers between devices  28.4 us (26%)
  Pallas kernels  3.78 us (4%)
  other arithmetic  2.39 us (2%)
  local copies, waits for them, and re-layouts  2.08 us (2%)
  between operations  1.63 us (2%)
    dot_general x77, matrix products, dot(): return jnp.dot(a, b, preferred_element_type=F32).astype(kind)  37.1 us
    ppermute x26, starting transfers between devices, send(): return lax.ppermute(value, BOTH, pairs)  32 us
    ppermute x26, waiting for transfers between devices, send(): return lax.ppermute(value, BOTH, pairs)  28.4 us
    pallas_call x4, Pallas kernels, call(): pl.pallas_call(kernel, out_shape=outs, grid_spec=pltpu.PrefetchScalarGrid...  3.78 us
  transfers between devices with their start and end apart: 32, of which 10 were waited for; matrix products, arithmetic and copies ran while one was open for 36% of the time, Pallas kernels for 4%

profile of v2, /device:TPU:0, one launch (start us, length us, event | category | flops | bytes accessed | tf_op | source)
XLA Modules:
  0.0 107.8 jit_solution(4908182966264880858)
XLA Ops:
  0.0 3.1 %collective-permute-start.2 = (bf16[64,2560]{1,0:T(8,128)(2,1)}, bf16[64,2560]{1,0:T(8,128)(2,1)S(1)}, u32[]{:S(2)}, u32[]{:S(2)}) collective-permute-start(bf16[64,2560]{1,0:T(8,128)(2,1)} %param.11), channel_id=1, source_target_pairs={{0,8},{1,9},{2,10},{3,11},{4,12},{5,13},{6,14},{7,15},{8,16},{9,17... | collective-permute-start | bytes 983048 | tf_op jit(solution)/shard_map/ring1/ppermute | solution.py:179
  3.1 1.5 %collective-permute-start.5 = (bf16[64,2560]{1,0:T(8,128)(2,1)}, bf16[64,2560]{1,0:T(8,128)(2,1)S(1)}, u32[]{:S(2)}, u32[]{:S(2)}) collective-permute-start(bf16[64,2560]{1,0:T(8,128)(2,1)} %param.11), channel_id=1, source_target_pairs={{0,4},{1,3},{2,6},{3,1},{4,0},{5,7},{6,2},{7,5},{8,12},{9,11},{10,... | collective-permute-start | bytes 983048 | tf_op jit(solution)/shard_map/near0/ppermute | solution.py:179
  7.9 3.1 %collective-permute-done = f32[16,64]{1,0:T(8,128)S(1)} collective-permute-done((f32[16,64]{1,0:T(8,128)S(1)}, f32[16,64]{1,0:T(8,128)S(1)}, u32[]{:S(2)}, u32[]{:S(2)}) %collective-permute-start) | collective-permute-done | bytes 4128 | tf_op jit(solution)/shard_map/tnear/ppermute | solution.py:179
  11.0 1.6 %collective-permute-start.1 = (f32[16,128]{1,0:T(8,128)S(1)}, f32[16,128]{1,0:T(8,128)S(1)}, u32[]{:S(2)}, u32[]{:S(2)}) collective-permute-start(f32[16,128]{1,0:T(8,128)S(1)} %pad_maximum_fusion.3.table_ref), channel_id=1, source_target_pairs={{0,8},{1,9},{2,10},{3,11},{4,12},{5,13},{6,14},{7,15},{8,16},{9,17... | collective-permute-start | bytes 24584 | tf_op jit(solution)/shard_map/turn1/ppermute | solution.py:179
  17.0 1.6 %collective-permute-start.4 = (bf16[64,2560]{1,0:T(8,128)(2,1)S(1)}, bf16[64,2560]{1,0:T(8,128)(2,1)S(1)}, u32[]{:S(2)}, u32[]{:S(2)}) collective-permute-start(bf16[64,2560]{1,0:T(8,128)(2,1)S(1)} %collective-permute-done.2), channel_id=1, source_target_pairs={{0,8},{1,9},{2,10},{3,11},{4,12},{5,13},{6,14},{7,15},{8,16},{9,17... | collective-permute-start | bytes 983048 | tf_op jit(solution)/shard_map/ring2/ppermute | solution.py:179
  19.1 1.6 %collective-permute-start.19 = (bf16[72,2560]{1,0:T(8,128)(2,1)S(1)}, bf16[72,2560]{1,0:T(8,128)(2,1)S(1)}, u32[]{:S(2)}, u32[]{:S(2)}) collective-permute-start(bf16[72,2560]{1,0:T(8,128)(2,1)S(1)} %fusion.63), channel_id=1, source_target_pairs={{0,2},{1,5},{2,0},{3,7},{4,6},{5,1},{6,4},{7,3},{8,10},{9,13},{10,... | collective-permute-start | bytes 1105928 | tf_op jit(solution)/shard_map/far0/ppermute | solution.py:179
  22.0 4.7 %collective-permute-done.6 = bf16[64,2560]{1,0:T(8,128)(2,1)S(1)} collective-permute-done((bf16[64,2560]{1,0:T(8,128)(2,1)S(1)}, bf16[64,2560]{1,0:T(8,128)(2,1)S(1)}, u32[]{:S(2)}, u32[]{:S(2)}) %collective-permute-start.6) | collective-permute-done | bytes 327712 | tf_op jit(solution)/shard_map/near1/ppermute | solution.py:179
  27.2 1.6 %collective-permute-start.9 = (bf16[72,2560]{1,0:T(8,128)(2,1)S(1)}, bf16[72,2560]{1,0:T(8,128)(2,1)S(1)}, u32[]{:S(2)}, u32[]{:S(2)}) collective-permute-start(bf16[72,2560]{1,0:T(8,128)(2,1)S(1)} %fusion.64), channel_id=1, source_target_pairs={{0,2},{1,5},{2,0},{3,7},{4,6},{5,1},{6,4},{7,3},{8,10},{9,13},{10,... | collective-permute-start | bytes 1105928 | tf_op jit(solution)/shard_map/far1/ppermute | solution.py:179
  29.7 1.6 %collective-permute-start.8 = (bf16[64,2560]{1,0:T(8,128)(2,1)S(1)}, bf16[64,2560]{1,0:T(8,128)(2,1)S(1)}, u32[]{:S(2)}, u32[]{:S(2)}) collective-permute-start(bf16[64,2560]{1,0:T(8,128)(2,1)S(1)} %collective-permute-done.4), channel_id=1, source_target_pairs={{0,8},{1,9},{2,10},{3,11},{4,12},{5,13},{6,14},{7,15},{8,16},{9,17... | collective-permute-start | bytes 983048 | tf_op jit(solution)/shard_map/ring3/ppermute | solution.py:179
  32.5 2.3 %collective-permute-done.9 = bf16[72,2560]{1,0:T(8,128)(2,1)S(1)} collective-permute-done((bf16[72,2560]{1,0:T(8,128)(2,1)S(1)}, bf16[72,2560]{1,0:T(8,128)(2,1)S(1)}, u32[]{:S(2)}, u32[]{:S(2)}) %collective-permute-start.9) | collective-permute-done | bytes 368672 | tf_op jit(solution)/shard_map/far1/ppermute | solution.py:179
  39.1 1.6 %collective-permute-start.12 = (bf16[72,2560]{1,0:T(8,128)(2,1)S(1)}, bf16[72,2560]{1,0:T(8,128)(2,1)S(1)}, u32[]{:S(2)}, u32[]{:S(2)}) collective-permute-start(bf16[72,2560]{1,0:T(8,128)(2,1)S(1)} %fusion.66), channel_id=1, source_target_pairs={{0,2},{1,5},{2,0},{3,7},{4,6},{5,1},{6,4},{7,3},{8,10},{9,13},{10,... | collective-permute-start | bytes 1105928 | tf_op jit(solution)/shard_map/far2/ppermute | solution.py:179
  48.7 1.5 %collective-permute-start.18 = (bf16[72,2560]{1,0:T(8,128)(2,1)S(1)}, bf16[72,2560]{1,0:T(8,128)(2,1)S(1)}, u32[]{:S(2)}, u32[]{:S(2)}) collective-permute-start(bf16[72,2560]{1,0:T(8,128)(2,1)S(1)} %slice.280), channel_id=1, source_target_pairs={{0,2},{1,5},{2,0},{3,7},{4,6},{5,1},{6,4},{7,3},{8,10},{9,13},{10,... | collective-permute-start | bytes 1105928 | tf_op jit(solution)/shard_map/back1/ppermute | solution.py:179
  61.1 1.4 %collective-permute-start.23 = (bf16[72,2560]{1,0:T(8,128)(2,1)S(1)}, bf16[72,2560]{1,0:T(8,128)(2,1)S(1)}, u32[]{:S(2)}, u32[]{:S(2)}) collective-permute-start(bf16[72,2560]{1,0:T(8,128)(2,1)S(1)} %slice.282), channel_id=1, source_target_pairs={{0,2},{1,5},{2,0},{3,7},{4,6},{5,1},{6,4},{7,3},{8,10},{9,13},{10,... | collective-permute-start | bytes 1105928 | tf_op jit(solution)/shard_map/back2/ppermute | solution.py:179
  63.8 1.3 %fusion.25 = f32[288,768]{1,0:T(8,128)S(1)} fusion(bf16[288,2560]{1,0:T(8,128)(2,1)S(1)} %pad_maximum_fusion, bf16[1,5120,768]{2,1,0:T(8,128)(2,1)S(1)} %copy-done, s32[]{:T(128)S(6)} %select_n.20), kind=kOutput, calls=%fused_computation.28 | convolution fusion | flops 1132462080 | bytes 6291460 | tf_op jit(solution)/shard_map/dot_general | solution.py:154
  67.7 1.7 %collective-permute-start.27 = (bf16[64,2560]{1,0:T(8,128)(2,1)S(1)}, bf16[64,2560]{1,0:T(8,128)(2,1)S(1)}, u32[]{:S(2)}, u32[]{:S(2)}) collective-permute-start(bf16[64,2560]{1,0:T(8,128)(2,1)S(1)} %fusion.71), channel_id=1, source_target_pairs={{0,8},{1,9},{2,10},{3,11},{4,12},{5,13},{6,14},{7,15},{8,16},{9,17... | collective-permute-start | bytes 983048 | tf_op jit(solution)/shard_map/add2/ppermute | solution.py:179
  69.8 1.3 %fusion.97 = f32[288,768]{1,0:T(8,128)S(1)} fusion(f32[288,768]{1,0:T(8,128)S(1)} %fusion.31, bf16[288,2560]{1,0:T(8,128)(2,1)S(1)} %collective-permute-done.20, bf16[1,5120,768]{2,1,0:T(8,128)(2,1)S(1)} %bitcast.159, s32[]{:T(128)S(6)} %select_n.21), kind=kOutput, calls=%fused_computation.127 | convolution fusion | flops 1132683264 | bytes 7176196 | tf_op jit(solution)/shard_map/dot_general | solution.py:154
  71.2 1.4 %multiply_convert_fusion = bf16[288,768]{1,0:T(8,128)(2,1)S(1)} fusion(f32[288,768]{1,0:T(8,128)S(1)} %fusion.97, f32[288,768]{1,0:T(8,128)S(1)} %fusion.25, bf16[288,2560]{1,0:T(8,128)(2,1)S(1)} %collective-permute-done.20, bf16[1,5120,768]{2,1,0:T(8,128)(2,1)S(1)} %copy-done, s32[]{:T(128)S(6)} %select_n.21), kind=kOutput, calls=%fused_computation.138 | convolution fusion | flops 1133789184 | bytes 7618564 | tf_op jit(solution)/shard_map/dot_general | solution.py:154
  73.1 1.4 %convolution_convert_fusion = bf16[288,2560]{1,0:T(8,128)(2,1)S(1)} fusion(bf16[288,768]{0,1:T(8,128)(2,1)S(1)} %fusion.103, bf16[1,768,5120]{2,1,0:T(8,128)(2,1)S(1)} %bitcast.157, s32[]{:T(128)S(6)} %select_n.21), kind=kOutput, calls=%fused_computation.4 | convolution fusion | flops 1133199360 | bytes 5996548 | tf_op jit(solution)/shard_map/dot_general | solution.py:154
  76.9 1.3 %fusion.2 = f32[288,2560]{1,0:T(8,128)S(1)} fusion(bf16[288,768]{1,0:T(8,128)(2,1)S(1)} %multiply_convert_fusion, bf16[1,768,5120]{2,1,0:T(8,128)(2,1)S(1)} %bitcast.157, s32[]{:T(128)S(6)} %select_n.20), kind=kOutput, calls=%fused_computation.5 | convolution fusion | flops 1132462080 | bytes 7323652 | tf_op jit(solution)/shard_map/dot_general | solution.py:154
  79.4 2.5 %collective-permute-start.25 = (bf16[72,2560]{1,0:T(8,128)(2,1)S(1)}, bf16[72,2560]{1,0:T(8,128)(2,1)S(1)}, u32[]{:S(2)}, u32[]{:S(2)}) collective-permute-start(bf16[72,2560]{1,0:T(8,128)(2,1)S(1)} %get-tuple-element.113), channel_id=1, source_target_pairs={{0,2},{1,5},{2,0},{3,7},{4,6},{5,1},{6,4},{7,3},{8,10},{9,13},{10,... | collective-permute-start | bytes 1105928 | tf_op jit(solution)/shard_map/back3/ppermute | solution.py:179
  84.9 2.4 %collective-permute-done.25 = bf16[72,2560]{1,0:T(8,128)(2,1)S(1)} collective-permute-done((bf16[72,2560]{1,0:T(8,128)(2,1)S(1)}, bf16[72,2560]{1,0:T(8,128)(2,1)S(1)}, u32[]{:S(2)}, u32[]{:S(2)}) %collective-permute-start.25) | collective-permute-done | bytes 368672 | tf_op jit(solution)/shard_map/back3/ppermute | solution.py:179
  89.4 5.7 %collective-permute-done.28 = bf16[64,2560]{1,0:T(8,128)(2,1)S(1)} collective-permute-done((bf16[64,2560]{1,0:T(8,128)(2,1)S(1)}, bf16[64,2560]{1,0:T(8,128)(2,1)S(1)}, u32[]{:S(2)}, u32[]{:S(2)}) %collective-permute-start.28) | collective-permute-done | bytes 327712 | tf_op jit(solution)/shard_map/sum3/ppermute | solution.py:179
  98.6 5.5 %collective-permute-done.30 = bf16[64,2560]{1,0:T(8,128)(2,1)S(1)} collective-permute-done((bf16[64,2560]{1,0:T(8,128)(2,1)S(1)}, bf16[64,2560]{1,0:T(8,128)(2,1)S(1)}, u32[]{:S(2)}, u32[]{:S(2)}) %collective-permute-start.30) | collective-permute-done | bytes 327712 | tf_op jit(solution)/shard_map/sum0/ppermute | solution.py:179
  104.1 2.6 %collective-permute-done.31 = bf16[64,2560]{1,0:T(8,128)(2,1)S(1)} collective-permute-done((bf16[64,2560]{1,0:T(8,128)(2,1)S(1)}, bf16[64,2560]{1,0:T(8,128)(2,1)S(1)}, u32[]{:S(2)}, u32[]{:S(2)}) %collective-permute-start.31) | collective-permute-done | bytes 327712 | tf_op jit(solution)/shard_map/add4/ppermute | solution.py:179
  (166 shorter events, 52.1 us)
Async XLA Ops:
  0.0 16.0 %collective-permute-start.2 = (bf16[64,2560]{1,0:T(8,128)(2,1)}, bf16[64,2560]{1,0:T(8,128)(2,1)S(1)}, u32[]{:S(2)}, u32[]{:S(2)}) collective-permute-start(bf16[64,2560]{1,0:T(8,128)(2,1)} %param.11), channel_id=1, source_target_pairs={{0,8},{1,9},{2,10},{3,11},{4,12},{5,13},{6,14},{7,15},{8,16},{9,17... | collective-permute-start | bytes 983048 | tf_op jit(solution)/shard_map/ring1/ppermute | solution.py:179
  3.1 15.6 %collective-permute-start.5 = (bf16[64,2560]{1,0:T(8,128)(2,1)}, bf16[64,2560]{1,0:T(8,128)(2,1)S(1)}, u32[]{:S(2)}, u32[]{:S(2)}) collective-permute-start(bf16[64,2560]{1,0:T(8,128)(2,1)} %param.11), channel_id=1, source_target_pairs={{0,4},{1,3},{2,6},{3,1},{4,0},{5,7},{6,2},{7,5},{8,12},{9,11},{10,... | collective-permute-start | bytes 983048 | tf_op jit(solution)/shard_map/near0/ppermute | solution.py:179
  11.0 7.6 %collective-permute-start.1 = (f32[16,128]{1,0:T(8,128)S(1)}, f32[16,128]{1,0:T(8,128)S(1)}, u32[]{:S(2)}, u32[]{:S(2)}) collective-permute-start(f32[16,128]{1,0:T(8,128)S(1)} %pad_maximum_fusion.3.table_ref), channel_id=1, source_target_pairs={{0,8},{1,9},{2,10},{3,11},{4,12},{5,13},{6,14},{7,15},{8,16},{9,17... | collective-permute-start | bytes 24584 | tf_op jit(solution)/shard_map/turn1/ppermute | solution.py:179
  16.0 10.7 %collective-permute-start.6 = (bf16[64,2560]{1,0:T(8,128)(2,1)S(1)}, bf16[64,2560]{1,0:T(8,128)(2,1)S(1)}, u32[]{:S(2)}, u32[]{:S(2)}) collective-permute-start(bf16[64,2560]{1,0:T(8,128)(2,1)S(1)} %collective-permute-done.2), channel_id=1, source_target_pairs={{0,4},{1,3},{2,6},{3,1},{4,0},{5,7},{6,2},{7,5},{8,12},{9,11},{10,... | collective-permute-start | bytes 983048 | tf_op jit(solution)/shard_map/near1/ppermute | solution.py:179
  17.0 11.7 %collective-permute-start.4 = (bf16[64,2560]{1,0:T(8,128)(2,1)S(1)}, bf16[64,2560]{1,0:T(8,128)(2,1)S(1)}, u32[]{:S(2)}, u32[]{:S(2)}) collective-permute-start(bf16[64,2560]{1,0:T(8,128)(2,1)S(1)} %collective-permute-done.2), channel_id=1, source_target_pairs={{0,8},{1,9},{2,10},{3,11},{4,12},{5,13},{6,14},{7,15},{8,16},{9,17... | collective-permute-start | bytes 983048 | tf_op jit(solution)/shard_map/ring2/ppermute | solution.py:179
  18.6 13.2 %collective-permute-start.3 = (f32[16,128]{1,0:T(8,128)S(1)}, f32[16,128]{1,0:T(8,128)S(1)}, u32[]{:S(2)}, u32[]{:S(2)}) collective-permute-start(f32[16,128]{1,0:T(8,128)S(1)} %collective-permute-done.1.table_ref), channel_id=1, source_target_pairs={{0,8},{1,9},{2,10},{3,11},{4,12},{5,13},{6,14},{7,15},{8,16},{9,17... | collective-permute-start | bytes 24584 | tf_op jit(solution)/shard_map/turn2/ppermute | solution.py:179
  19.1 43.4 %collective-permute-start.19 = (bf16[72,2560]{1,0:T(8,128)(2,1)S(1)}, bf16[72,2560]{1,0:T(8,128)(2,1)S(1)}, u32[]{:S(2)}, u32[]{:S(2)}) collective-permute-start(bf16[72,2560]{1,0:T(8,128)(2,1)S(1)} %fusion.63), channel_id=1, source_target_pairs={{0,2},{1,5},{2,0},{3,7},{4,6},{5,1},{6,4},{7,3},{8,10},{9,13},{10,... | collective-permute-start | bytes 1105928 | tf_op jit(solution)/shard_map/far0/ppermute | solution.py:179
  27.2 7.6 %collective-permute-start.9 = (bf16[72,2560]{1,0:T(8,128)(2,1)S(1)}, bf16[72,2560]{1,0:T(8,128)(2,1)S(1)}, u32[]{:S(2)}, u32[]{:S(2)}) collective-permute-start(bf16[72,2560]{1,0:T(8,128)(2,1)S(1)} %fusion.64), channel_id=1, source_target_pairs={{0,2},{1,5},{2,0},{3,7},{4,6},{5,1},{6,4},{7,3},{8,10},{9,13},{10,... | collective-permute-start | bytes 1105928 | tf_op jit(solution)/shard_map/far1/ppermute | solution.py:179
  28.7 9.8 %collective-permute-start.11 = (bf16[64,2560]{1,0:T(8,128)(2,1)S(1)}, bf16[64,2560]{1,0:T(8,128)(2,1)S(1)}, u32[]{:S(2)}, u32[]{:S(2)}) collective-permute-start(bf16[64,2560]{1,0:T(8,128)(2,1)S(1)} %collective-permute-done.4), channel_id=1, source_target_pairs={{0,4},{1,3},{2,6},{3,1},{4,0},{5,7},{6,2},{7,5},{8,12},{9,11},{10,... | collective-permute-start | bytes 983048 | tf_op jit(solution)/shard_map/near2/ppermute | solution.py:179
  29.7 15.0 %collective-permute-start.8 = (bf16[64,2560]{1,0:T(8,128)(2,1)S(1)}, bf16[64,2560]{1,0:T(8,128)(2,1)S(1)}, u32[]{:S(2)}, u32[]{:S(2)}) collective-permute-start(bf16[64,2560]{1,0:T(8,128)(2,1)S(1)} %collective-permute-done.4), channel_id=1, source_target_pairs={{0,8},{1,9},{2,10},{3,11},{4,12},{5,13},{6,14},{7,15},{8,16},{9,17... | collective-permute-start | bytes 983048 | tf_op jit(solution)/shard_map/ring3/ppermute | solution.py:179
  31.9 13.9 %collective-permute-start.7 = (f32[16,128]{1,0:T(8,128)S(1)}, f32[16,128]{1,0:T(8,128)S(1)}, u32[]{:S(2)}, u32[]{:S(2)}) collective-permute-start(f32[16,128]{1,0:T(8,128)S(1)} %collective-permute-done.3.table_ref), channel_id=1, source_target_pairs={{0,8},{1,9},{2,10},{3,11},{4,12},{5,13},{6,14},{7,15},{8,16},{9,17... | collective-permute-start | bytes 24584 | tf_op jit(solution)/shard_map/turn3/ppermute | solution.py:179
  39.1 7.6 %collective-permute-start.12 = (bf16[72,2560]{1,0:T(8,128)(2,1)S(1)}, bf16[72,2560]{1,0:T(8,128)(2,1)S(1)}, u32[]{:S(2)}, u32[]{:S(2)}) collective-permute-start(bf16[72,2560]{1,0:T(8,128)(2,1)S(1)} %fusion.66), channel_id=1, source_target_pairs={{0,2},{1,5},{2,0},{3,7},{4,6},{5,1},{6,4},{7,3},{8,10},{9,13},{10,... | collective-permute-start | bytes 1105928 | tf_op jit(solution)/shard_map/far2/ppermute | solution.py:179
  44.7 7.2 %collective-permute-start.14 = (bf16[64,2560]{1,0:T(8,128)(2,1)S(1)}, bf16[64,2560]{1,0:T(8,128)(2,1)S(1)}, u32[]{:S(2)}, u32[]{:S(2)}) collective-permute-start(bf16[64,2560]{1,0:T(8,128)(2,1)S(1)} %collective-permute-done.8), channel_id=1, source_target_pairs={{0,4},{1,3},{2,6},{3,1},{4,0},{5,7},{6,2},{7,5},{8,12},{9,11},{10,... | collective-permute-start | bytes 983048 | tf_op jit(solution)/shard_map/near3/ppermute | solution.py:179
  48.7 9.4 %collective-permute-start.18 = (bf16[72,2560]{1,0:T(8,128)(2,1)S(1)}, bf16[72,2560]{1,0:T(8,128)(2,1)S(1)}, u32[]{:S(2)}, u32[]{:S(2)}) collective-permute-start(bf16[72,2560]{1,0:T(8,128)(2,1)S(1)} %slice.280), channel_id=1, source_target_pairs={{0,2},{1,5},{2,0},{3,7},{4,6},{5,1},{6,4},{7,3},{8,10},{9,13},{10,... | collective-permute-start | bytes 1105928 | tf_op jit(solution)/shard_map/back1/ppermute | solution.py:179
  53.4 9.1 %collective-permute-start.15 = (bf16[72,2560]{1,0:T(8,128)(2,1)S(1)}, bf16[72,2560]{1,0:T(8,128)(2,1)S(1)}, u32[]{:S(2)}, u32[]{:S(2)}) collective-permute-start(bf16[72,2560]{1,0:T(8,128)(2,1)S(1)} %fusion.70), channel_id=1, source_target_pairs={{0,2},{1,5},{2,0},{3,7},{4,6},{5,1},{6,4},{7,3},{8,10},{9,13},{10,... | collective-permute-start | bytes 1105928 | tf_op jit(solution)/shard_map/far3/ppermute | solution.py:179
  58.7 8.7 %collective-permute-start.21 = (bf16[64,2560]{1,0:T(8,128)(2,1)S(1)}, bf16[64,2560]{1,0:T(8,128)(2,1)S(1)}, u32[]{:S(2)}, u32[]{:S(2)}) collective-permute-start(bf16[64,2560]{1,0:T(8,128)(2,1)S(1)} %fusion.75), channel_id=1, source_target_pairs={{0,4},{1,3},{2,6},{3,1},{4,0},{5,7},{6,2},{7,5},{8,12},{9,11},{10,... | collective-permute-start | bytes 983048 | tf_op jit(solution)/shard_map/sum1/ppermute | solution.py:179
  61.1 14.0 %collective-permute-start.23 = (bf16[72,2560]{1,0:T(8,128)(2,1)S(1)}, bf16[72,2560]{1,0:T(8,128)(2,1)S(1)}, u32[]{:S(2)}, u32[]{:S(2)}) collective-permute-start(bf16[72,2560]{1,0:T(8,128)(2,1)S(1)} %slice.282), channel_id=1, source_target_pairs={{0,2},{1,5},{2,0},{3,7},{4,6},{5,1},{6,4},{7,3},{8,10},{9,13},{10,... | collective-permute-start | bytes 1105928 | tf_op jit(solution)/shard_map/back2/ppermute | solution.py:179
  67.7 15.3 %collective-permute-start.27 = (bf16[64,2560]{1,0:T(8,128)(2,1)S(1)}, bf16[64,2560]{1,0:T(8,128)(2,1)S(1)}, u32[]{:S(2)}, u32[]{:S(2)}) collective-permute-start(bf16[64,2560]{1,0:T(8,128)(2,1)S(1)} %fusion.71), channel_id=1, source_target_pairs={{0,8},{1,9},{2,10},{3,11},{4,12},{5,13},{6,14},{7,15},{8,16},{9,17... | collective-permute-start | bytes 983048 | tf_op jit(solution)/shard_map/add2/ppermute | solution.py:179
  75.6 7.1 %collective-permute-start.26 = (bf16[64,2560]{1,0:T(8,128)(2,1)S(1)}, bf16[64,2560]{1,0:T(8,128)(2,1)S(1)}, u32[]{:S(2)}, u32[]{:S(2)}) collective-permute-start(bf16[64,2560]{1,0:T(8,128)(2,1)S(1)} %fusion.76), channel_id=1, source_target_pairs={{0,4},{1,3},{2,6},{3,1},{4,0},{5,7},{6,2},{7,5},{8,12},{9,11},{10,... | collective-permute-start | bytes 983048 | tf_op jit(solution)/shard_map/sum2/ppermute | solution.py:179
  79.4 7.9 %collective-permute-start.25 = (bf16[72,2560]{1,0:T(8,128)(2,1)S(1)}, bf16[72,2560]{1,0:T(8,128)(2,1)S(1)}, u32[]{:S(2)}, u32[]{:S(2)}) collective-permute-start(bf16[72,2560]{1,0:T(8,128)(2,1)S(1)} %get-tuple-element.113), channel_id=1, source_target_pairs={{0,2},{1,5},{2,0},{3,7},{4,6},{5,1},{6,4},{7,3},{8,10},{9,13},{10,... | collective-permute-start | bytes 1105928 | tf_op jit(solution)/shard_map/back3/ppermute | solution.py:179
  81.8 14.6 %collective-permute-start.24 = (bf16[72,2560]{1,0:T(8,128)(2,1)S(1)}, bf16[72,2560]{1,0:T(8,128)(2,1)S(1)}, u32[]{:S(2)}, u32[]{:S(2)}) collective-permute-start(bf16[72,2560]{1,0:T(8,128)(2,1)S(1)} %get-tuple-element.111), channel_id=1, source_target_pairs={{0,2},{1,5},{2,0},{3,7},{4,6},{5,1},{6,4},{7,3},{8,10},{9,13},{10,... | collective-permute-start | bytes 1105928 | tf_op jit(solution)/shard_map/back0/ppermute | solution.py:179
  83.4 11.7 %collective-permute-start.29 = (bf16[64,2560]{1,0:T(8,128)(2,1)S(1)}, bf16[64,2560]{1,0:T(8,128)(2,1)S(1)}, u32[]{:S(2)}, u32[]{:S(2)}) collective-permute-start(bf16[64,2560]{1,0:T(8,128)(2,1)S(1)} %fusion.72), channel_id=1, source_target_pairs={{0,8},{1,9},{2,10},{3,11},{4,12},{5,13},{6,14},{7,15},{8,16},{9,17... | collective-permute-start | bytes 983048 | tf_op jit(solution)/shard_map/add3/ppermute | solution.py:179
  87.9 7.1 %collective-permute-start.28 = (bf16[64,2560]{1,0:T(8,128)(2,1)S(1)}, bf16[64,2560]{1,0:T(8,128)(2,1)S(1)}, u32[]{:S(2)}, u32[]{:S(2)}) collective-permute-start(bf16[64,2560]{1,0:T(8,128)(2,1)S(1)} %fusion.77), channel_id=1, source_target_pairs={{0,4},{1,3},{2,6},{3,1},{4,0},{5,7},{6,2},{7,5},{8,12},{9,11},{10,... | collective-permute-start | bytes 983048 | tf_op jit(solution)/shard_map/sum3/ppermute | solution.py:179
  95.4 11.3 %collective-permute-start.31 = (bf16[64,2560]{1,0:T(8,128)(2,1)S(1)}, bf16[64,2560]{1,0:T(8,128)(2,1)S(1)}, u32[]{:S(2)}, u32[]{:S(2)}) collective-permute-start(bf16[64,2560]{1,0:T(8,128)(2,1)S(1)} %fusion.73), channel_id=1, source_target_pairs={{0,8},{1,9},{2,10},{3,11},{4,12},{5,13},{6,14},{7,15},{8,16},{9,17... | collective-permute-start | bytes 983048 | tf_op jit(solution)/shard_map/add4/ppermute | solution.py:179
  (21 other events, 93.5 us)

commit v3 on v2

--- a/solution.py
+++ b/solution.py
@@ -154,6 +154,27 @@
     return jnp.dot(a, b, preferred_element_type=F32).astype(kind)
 
 
+def stage_order(ring):
+    end = ring - 1
+    plan = [("spread", 0), ("spread", 1), ("route", 1), ("select", 1), ("spread", 2)]
+    plan += [("route", 0), ("select", 0)]
+    for k in range(1, ring):
+        plan += [("rows", [k]), ("own_half", [k])]
+        if k < end:
+            plan += [("route", k + 1), ("select", k + 1)]
+        if k > 1:
+            plan += [("merge", k - 1)]
+        plan += [("peer_half", [k])]
+        if k + 1 < end:
+            plan += [("spread", k + 2)]
+        plan += [("finish", [k])]
+        if 1 < k < end:
+            plan += [("pass_on", k - 1)]
+    plan += [("rows", [0]), ("own_half", [0]), ("pass_on", end - 1), ("peer_half", [0])]
+    plan += [("merge", end), ("finish", [0]), ("pass_on", end), ("merge", 0)]
+    return plan + [("pass_on", ring)]
+
+
 def tree_body(tokens, w_gate, w_up, w_down, route_ids, route_weight, live_count, owner_slot):
     tok_dev, top = route_ids.shape
     width = tokens.shape[1]
@@ -174,12 +195,11 @@
     far = [(2 * e + c, 2 * (e ^ bits[c][1]) + c) for e, c in cells]
     scalars = jnp.stack([me, me ^ jnp.where(core == 0, bits[0][1], bits[1][1]), core])
 
-    def send(name, value, pairs):
-        with jax.named_scope(name):
-            return lax.ppermute(value, BOTH, pairs)
+    def send(value, pairs):
+        return lax.ppermute(value, BOTH, pairs)
 
     def swap(value):
-        return lax.ppermute(value, "tensor", [(0, 1), (1, 0)])
+        return send(value, [(2 * e + c, 2 * e + 1 - c) for e, c in cells])
 
     def after(value, *events):
         return lax.optimization_barrier((value, *events))[0]
@@ -195,11 +215,12 @@
         ],
         1,
     ).T
+
     def halves(w, dim):
         return [lax.dynamic_slice_in_dim(w[0], c * width, width, dim) for c in (core, 1 - core)]
 
     gates, ups, downs = halves(w_gate, 0), halves(w_up, 0), halves(w_down, 1)
-    blocks, tables, beside, made, sent, got = {}, {}, {}, {}, {}, {}
+    blocks, tables, beside, made, sent, kept, got = {}, {}, {}, {}, {}, {}, {}
     arriving, state, back, partial, own_sum, near_sum = {}, {}, {}, {}, {}, {}
     last = []
 
@@ -217,14 +238,14 @@
     def spread(k):
         blocks[k] = done(then(arriving[k])) if k else tokens
         if k + 1 < ring:
-            arriving[k + 1] = send(f"ring{k + 1}", blocks[k], turn(1))
-        beside[k] = send(f"near{k}", blocks[k], near)
+            arriving[k + 1] = send(blocks[k], turn(1))
+        beside[k] = send(blocks[k], near)
         if k:
             tables[k] = after(tables[k], blocks[k])
         else:
-            tables[0] = jnp.concatenate([table, send("tnear", table, near)], 1)
+            tables[0] = jnp.concatenate([table, send(table, near)], 1)
         if k + 1 < ring:
-            tables[k + 1] = send(f"turn{k + 1}", tables[k], turn(1))
+            tables[k + 1] = send(tables[k], turn(1))
 
     def route(k):
         made[k] = routing(scalars, top, capacity, then(tables[k]))
@@ -232,12 +253,13 @@
 
     def select(k):
         beside[k] = then(beside[k])
-        sent[k] = done(pick(made[k][0], k))
-        got[k] = send(f"far{k}", sent[k], far)
+        kept[k] = done(pick(made[k][1], k))
+        sent[k] = done(pick(then(made[k][0]), k))
+        got[k] = send(sent[k], far)
 
     def rows(ks):
         cross = crossing(capacity, len(ks))
-        mine = jnp.concatenate([pick(made[k][1], k) for k in ks] + [then(got[k]) for k in ks])
+        mine = jnp.concatenate([kept[k] for k in ks] + [then(got[k]) for k in ks])
         state[ks[0]] = [mine, swap(done(dot(cross, mine, BF16))), cross]
 
     def own_half(ks):
@@ -260,7 +282,7 @@
         came = [out[(len(ks) + p) * count : (len(ks) + p + 1) * count] for p in range(len(ks))]
         came = done(lax.optimization_barrier(tuple(came)))
         for p, k in enumerate(ks):
-            back[k] = out[p * count : (p + 1) * count], send(f"back{k}", came[p], far)
+            back[k] = out[p * count : (p + 1) * count], send(came[p], far)
 
     def merge(k):
         high, low = made[k][2:]
@@ -271,34 +293,29 @@
             return dot(matrix[:, :count], stay) + dot(matrix[:, count : 2 * count], came)
 
         total = done((add(high[tok_dev:]) + add(low[tok_dev:])).astype(BF16))
-        near_sum[k] = send(f"sum{k}", total, near)
+        near_sum[k] = send(total, near)
         own_sum[k] = add(high[:tok_dev]) + add(low[:tok_dev])
 
     def pass_on(k):
         total = own_sum[k % ring] + then(near_sum[k % ring]).astype(F32)
         if k > 1:
-            total += partial[k - 1].astype(F32)
+            total = after(total) + partial[k - 1].astype(F32)
         total = done(total.astype(BF16))
-        partial[k] = send(f"add{k + 1}", total, turn(1)) if k < ring else total
-
-    passes = {k: [k] for k in range(1, ring - 1)}
-    passes[ring - 1] = [ring - 1, 0]
-    plan = [(spread, 0), (route, 0), (spread, 1), (select, 0), (route, 1), (select, 1), (spread, 2)]
-    for k, ks in passes.items():
-        plan += [(rows, ks), (own_half, ks)]
-        if k + 1 < ring:
-            plan += [(route, k + 1), (select, k + 1)]
-        if k > 2:
-            plan += [(pass_on, k - 2)]
-        plan += [(peer_half, ks)]
-        if k + 2 < ring:
-            plan += [(spread, k + 2)]
-        if k > 1:
-            plan += [(merge, k - 1)]
-        plan += [(finish, ks)]
-    plan += [(pass_on, ring - 2), (merge, ring - 1), (pass_on, ring - 1), (merge, 0)]
-    for stage, which in plan + [(pass_on, ring)]:
-        stage(which)
+        partial[k] = send(total, turn(1)) if k < ring else total
+
+    stages = dict(
+        spread=spread,
+        route=route,
+        select=select,
+        rows=rows,
+        own_half=own_half,
+        peer_half=peer_half,
+        finish=finish,
+        merge=merge,
+        pass_on=pass_on,
+    )
+    for stage, which in stage_order(ring):
+        stages[stage](which)
     return partial[ring]
 
 

time: 108 us -> 129 us (1.19)
  waiting for transfers between devices: 28.4 us -> 50.5 us
  matrix products: 37.1 us -> 34.4 us
    ppermute x26 -> x34, waiting for transfers between devices: 28.4 us -> 50.5 us  [send(): return lax.ppermute(value, BOTH, pairs)]
    dot_general x77 -> x84, matrix products: 37.1 us -> 34.4 us  [dot(): return jnp.dot(a, b, preferred_element_type=F32).astype(kind)]
    ppermute x26 -> x34, starting transfers between devices: 32 us -> 32.2 us  [send(): return lax.ppermute(value, BOTH, pairs)]
  transfers between devices with their start and end apart: 32 -> 34, of which waited for: 10 -> 13; matrix products, arithmetic and copies ran while one was open for 36% -> 29% of each run, Pallas kernels for 4% -> 3%
where the time goes in v3:
time: 129 us
  waiting for transfers between devices  50.5 us (39%)
  matrix products  34.4 us (27%)
  starting transfers between devices  32.2 us (25%)
  Pallas kernels  3.78 us (3%)
  other arithmetic  3.24 us (3%)
  local copies, waits for them, and re-layouts  2.78 us (2%)
  between operations  1.66 us (1%)
    ppermute x34, waiting for transfers between devices, send(): return lax.ppermute(value, BOTH, pairs)  50.5 us
    dot_general x84, matrix products, dot(): return jnp.dot(a, b, preferred_element_type=F32).astype(kind)  34.4 us
    ppermute x34, starting transfers between devices, send(): return lax.ppermute(value, BOTH, pairs)  32.2 us
    pallas_call x4, Pallas kernels, call(): pl.pallas_call(kernel, out_shape=outs, grid_spec=pltpu.PrefetchScalarGrid...  3.78 us
  transfers between devices with their start and end apart: 34, of which 13 were waited for; matrix products, arithmetic and copies ran while one was open for 29% of the time, Pallas kernels for 3%

profile of v3, /device:TPU:0, one launch (start us, length us, event | category | flops | bytes accessed | tf_op | source)
XLA Modules:
  0.0 128.7 jit_solution(13092256151880640852)
XLA Ops:
  0.0 3.1 %collective-permute-start.1 = (bf16[64,2560]{1,0:T(8,128)(2,1)}, bf16[64,2560]{1,0:T(8,128)(2,1)S(1)}, u32[]{:S(2)}, u32[]{:S(2)}) collective-permute-start(bf16[64,2560]{1,0:T(8,128)(2,1)} %param.12), channel_id=1, source_target_pairs={{0,8},{1,9},{2,10},{3,11},{4,12},{5,13},{6,14},{7,15},{8,16},{9,17... | collective-permute-start | bytes 983048 | tf_op jit(solution)/shard_map/ppermute | solution.py:199
  4.4 8.7 %collective-permute-done.1 = bf16[64,2560]{1,0:T(8,128)(2,1)S(1)} collective-permute-done((bf16[64,2560]{1,0:T(8,128)(2,1)}, bf16[64,2560]{1,0:T(8,128)(2,1)S(1)}, u32[]{:S(2)}, u32[]{:S(2)}) %collective-permute-start.1) | collective-permute-done | bytes 327712 | tf_op jit(solution)/shard_map/ppermute | solution.py:199
  13.1 1.5 %collective-permute-start.4 = (bf16[64,2560]{1,0:T(8,128)(2,1)S(1)}, bf16[64,2560]{1,0:T(8,128)(2,1)S(1)}, u32[]{:S(2)}, u32[]{:S(2)}) collective-permute-start(bf16[64,2560]{1,0:T(8,128)(2,1)S(1)} %collective-permute-done.1), channel_id=1, source_target_pairs={{0,4},{1,3},{2,6},{3,1},{4,0},{5,7},{6,2},{7,5},{8,12},{9,11},{10,... | collective-permute-start | bytes 983048 | tf_op jit(solution)/shard_map/ppermute | solution.py:199
  16.5 1.5 %collective-permute-start.5 = (bf16[64,2560]{1,0:T(8,128)(2,1)}, bf16[64,2560]{1,0:T(8,128)(2,1)S(1)}, u32[]{:S(2)}, u32[]{:S(2)}) collective-permute-start(bf16[64,2560]{1,0:T(8,128)(2,1)} %param.12), channel_id=1, source_target_pairs={{0,4},{1,3},{2,6},{3,1},{4,0},{5,7},{6,2},{7,5},{8,12},{9,11},{10,... | collective-permute-start | bytes 983048 | tf_op jit(solution)/shard_map/ppermute | solution.py:199
  18.0 2.2 %collective-permute-done = f32[16,64]{1,0:T(8,128)S(1)} collective-permute-done((f32[16,64]{1,0:T(8,128)S(1)}, f32[16,64]{1,0:T(8,128)S(1)}, u32[]{:S(2)}, u32[]{:S(2)}) %collective-permute-start) | collective-permute-done | bytes 4128 | tf_op jit(solution)/shard_map/ppermute | solution.py:199
  21.6 4.2 %collective-permute-done.3.table_ref = f32[16,128]{1,0:T(8,128)S(1)} collective-permute-done((f32[16,128]{1,0:T(8,128)S(1)}, f32[16,128]{1,0:T(8,128)S(1)}, u32[]{:S(2)}, u32[]{:S(2)}) %collective-permute-start.3) | collective-permute-done | bytes 8224 | tf_op jit(solution)/shard_map/ppermute | solution.py:199
  27.9 1.6 %collective-permute-start.10 = (bf16[72,2560]{1,0:T(8,128)(2,1)S(1)}, bf16[72,2560]{1,0:T(8,128)(2,1)S(1)}, u32[]{:S(2)}, u32[]{:S(2)}) collective-permute-start(bf16[72,2560]{1,0:T(8,128)(2,1)S(1)} %fusion.81), channel_id=1, source_target_pairs={{0,2},{1,5},{2,0},{3,7},{4,6},{5,1},{6,4},{7,3},{8,10},{9,13},{10,... | collective-permute-start | bytes 1105928 | tf_op jit(solution)/shard_map/ppermute | solution.py:199
  30.4 1.4 %collective-permute-start.12 = (bf16[64,2560]{1,0:T(8,128)(2,1)S(1)}, bf16[64,2560]{1,0:T(8,128)(2,1)S(1)}, u32[]{:S(2)}, u32[]{:S(2)}) collective-permute-start(bf16[64,2560]{1,0:T(8,128)(2,1)S(1)} %collective-permute-done.2), channel_id=1, source_target_pairs={{0,4},{1,3},{2,6},{3,1},{4,0},{5,7},{6,2},{7,5},{8,12},{9,11},{10,... | collective-permute-start | bytes 983048 | tf_op jit(solution)/shard_map/ppermute | solution.py:199
  34.7 1.6 %collective-permute-start.6 = (bf16[72,2560]{1,0:T(8,128)(2,1)S(1)}, bf16[72,2560]{1,0:T(8,128)(2,1)S(1)}, u32[]{:S(2)}, u32[]{:S(2)}) collective-permute-start(bf16[72,2560]{1,0:T(8,128)(2,1)S(1)} %fusion.83), channel_id=1, source_target_pairs={{0,2},{1,5},{2,0},{3,7},{4,6},{5,1},{6,4},{7,3},{8,10},{9,13},{10,... | collective-permute-start | bytes 1105928 | tf_op jit(solution)/shard_map/ppermute | solution.py:199
  36.6 1.3 collective-permute-done.10
  48.6 1.6 %collective-permute-start.15 = (bf16[64,2560]{1,0:T(8,128)(2,1)S(1)}, bf16[64,2560]{1,0:T(8,128)(2,1)S(1)}, u32[]{:S(2)}, u32[]{:S(2)}) collective-permute-start(bf16[64,2560]{1,0:T(8,128)(2,1)S(1)} %collective-permute-done.9), channel_id=1, source_target_pairs={{0,4},{1,3},{2,6},{3,1},{4,0},{5,7},{6,2},{7,5},{8,12},{9,11},{10,... | collective-permute-start | bytes 983048 | tf_op jit(solution)/shard_map/ppermute | solution.py:199
  51.7 5.9 %collective-permute-done.13 = bf16[72,2560]{1,0:T(8,128)(2,1)S(1)} collective-permute-done((bf16[72,2560]{1,0:T(8,128)(2,1)S(1)}, bf16[72,2560]{1,0:T(8,128)(2,1)S(1)}, u32[]{:S(2)}, u32[]{:S(2)}) %collective-permute-start.13) | collective-permute-done | bytes 368672 | tf_op jit(solution)/shard_map/ppermute | solution.py:199
  68.3 1.4 %collective-permute-start.18 = (bf16[64,2560]{1,0:T(8,128)(2,1)S(1)}, bf16[64,2560]{1,0:T(8,128)(2,1)S(1)}, u32[]{:S(2)}, u32[]{:S(2)}) collective-permute-start(bf16[64,2560]{1,0:T(8,128)(2,1)S(1)} %fusion.89), channel_id=1, source_target_pairs={{0,4},{1,3},{2,6},{3,1},{4,0},{5,7},{6,2},{7,5},{8,12},{9,11},{10,... | collective-permute-start | bytes 983048 | tf_op jit(solution)/shard_map/ppermute | solution.py:199
  70.9 4.5 %collective-permute-done.18 = bf16[64,2560]{1,0:T(8,128)(2,1)S(1)} collective-permute-done((bf16[64,2560]{1,0:T(8,128)(2,1)S(1)}, bf16[64,2560]{1,0:T(8,128)(2,1)S(1)}, u32[]{:S(2)}, u32[]{:S(2)}) %collective-permute-start.18) | collective-permute-done | bytes 327712 | tf_op jit(solution)/shard_map/ppermute | solution.py:199
  77.7 1.6 %collective-permute-start.22 = (bf16[72,2560]{1,0:T(8,128)(2,1)S(1)}, bf16[72,2560]{1,0:T(8,128)(2,1)S(1)}, u32[]{:S(2)}, u32[]{:S(2)}) collective-permute-start(bf16[72,2560]{1,0:T(8,128)(2,1)S(1)} %slice.282), channel_id=1, source_target_pairs={{0,2},{1,5},{2,0},{3,7},{4,6},{5,1},{6,4},{7,3},{8,10},{9,13},{10,... | collective-permute-start | bytes 1105928 | tf_op jit(solution)/shard_map/ppermute | solution.py:199
  80.4 4.9 %collective-permute-done.22 = bf16[72,2560]{1,0:T(8,128)(2,1)S(1)} collective-permute-done((bf16[72,2560]{1,0:T(8,128)(2,1)S(1)}, bf16[72,2560]{1,0:T(8,128)(2,1)S(1)}, u32[]{:S(2)}, u32[]{:S(2)}) %collective-permute-start.22) | collective-permute-done | bytes 368672 | tf_op jit(solution)/shard_map/ppermute | solution.py:199
  88.8 1.4 %collective-permute-start.25 = (bf16[64,2560]{1,0:T(8,128)(2,1)S(1)}, bf16[64,2560]{1,0:T(8,128)(2,1)S(1)}, u32[]{:S(2)}, u32[]{:S(2)}) collective-permute-start(bf16[64,2560]{1,0:T(8,128)(2,1)S(1)} %fusion.90), channel_id=1, source_target_pairs={{0,4},{1,3},{2,6},{3,1},{4,0},{5,7},{6,2},{7,5},{8,12},{9,11},{10,... | collective-permute-start | bytes 983048 | tf_op jit(solution)/shard_map/ppermute | solution.py:199
  94.6 2.8 %collective-permute-done.25 = bf16[64,2560]{1,0:T(8,128)(2,1)S(1)} collective-permute-done((bf16[64,2560]{1,0:T(8,128)(2,1)S(1)}, bf16[64,2560]{1,0:T(8,128)(2,1)S(1)}, u32[]{:S(2)}, u32[]{:S(2)}) %collective-permute-start.25) | collective-permute-done | bytes 327712 | tf_op jit(solution)/shard_map/ppermute | solution.py:199
  98.0 2.4 %collective-permute-start.31 = (bf16[64,2560]{1,0:T(8,128)(2,1)S(1)}, bf16[64,2560]{1,0:T(8,128)(2,1)S(1)}, u32[]{:S(2)}, u32[]{:S(2)}) collective-permute-start(bf16[64,2560]{1,0:T(8,128)(2,1)S(1)} %add_convert_fusion.6), channel_id=1, source_target_pairs={{0,8},{1,9},{2,10},{3,11},{4,12},{5,13},{6,14},{7,15},{8,16},{9,17... | collective-permute-start | bytes 983048 | tf_op jit(solution)/shard_map/ppermute | solution.py:199
  106.2 1.9 %collective-permute-start.29 = (bf16[72,2560]{1,0:T(8,128)(2,1)S(1)}, bf16[72,2560]{1,0:T(8,128)(2,1)S(1)}, u32[]{:S(2)}, u32[]{:S(2)}) collective-permute-start(bf16[72,2560]{1,0:T(8,128)(2,1)S(1)} %slice.287), channel_id=1, source_target_pairs={{0,2},{1,5},{2,0},{3,7},{4,6},{5,1},{6,4},{7,3},{8,10},{9,13},{10,... | collective-permute-start | bytes 1105928 | tf_op jit(solution)/shard_map/ppermute | solution.py:199
  108.1 6.0 %collective-permute-done.30 = bf16[64,2560]{1,0:T(8,128)(2,1)S(1)} collective-permute-done((bf16[64,2560]{1,0:T(8,128)(2,1)S(1)}, bf16[64,2560]{1,0:T(8,128)(2,1)S(1)}, u32[]{:S(2)}, u32[]{:S(2)}) %collective-permute-start.30) | collective-permute-done | bytes 327712 | tf_op jit(solution)/shard_map/ppermute | solution.py:199
  116.4 2.3 %collective-permute-start.33 = (bf16[64,2560]{1,0:T(8,128)(2,1)S(1)}, bf16[64,2560]{1,0:T(8,128)(2,1)S(1)}, u32[]{:S(2)}, u32[]{:S(2)}) collective-permute-start(bf16[64,2560]{1,0:T(8,128)(2,1)S(1)} %add_convert_fusion.5), channel_id=1, source_target_pairs={{0,8},{1,9},{2,10},{3,11},{4,12},{5,13},{6,14},{7,15},{8,16},{9,17... | collective-permute-start | bytes 983048 | tf_op jit(solution)/shard_map/ppermute | solution.py:199
  119.0 3.9 %collective-permute-done.32 = bf16[64,2560]{1,0:T(8,128)(2,1)S(1)} collective-permute-done((bf16[64,2560]{1,0:T(8,128)(2,1)S(1)}, bf16[64,2560]{1,0:T(8,128)(2,1)S(1)}, u32[]{:S(2)}, u32[]{:S(2)}) %collective-permute-start.32) | collective-permute-done | bytes 327712 | tf_op jit(solution)/shard_map/ppermute | solution.py:199
  123.2 4.7 %collective-permute-done.33 = bf16[64,2560]{1,0:T(8,128)(2,1)S(1)} collective-permute-done((bf16[64,2560]{1,0:T(8,128)(2,1)S(1)}, bf16[64,2560]{1,0:T(8,128)(2,1)S(1)}, u32[]{:S(2)}, u32[]{:S(2)}) %collective-permute-start.33) | collective-permute-done | bytes 327712 | tf_op jit(solution)/shard_map/ppermute | solution.py:199
  (175 shorter events, 54.8 us)
Async XLA Ops:
  0.0 13.1 %collective-permute-start.1 = (bf16[64,2560]{1,0:T(8,128)(2,1)}, bf16[64,2560]{1,0:T(8,128)(2,1)S(1)}, u32[]{:S(2)}, u32[]{:S(2)}) collective-permute-start(bf16[64,2560]{1,0:T(8,128)(2,1)} %param.12), channel_id=1, source_target_pairs={{0,8},{1,9},{2,10},{3,11},{4,12},{5,13},{6,14},{7,15},{8,16},{9,17... | collective-permute-start | bytes 983048 | tf_op jit(solution)/shard_map/ppermute | solution.py:199
  13.1 13.7 %collective-permute-start.4 = (bf16[64,2560]{1,0:T(8,128)(2,1)S(1)}, bf16[64,2560]{1,0:T(8,128)(2,1)S(1)}, u32[]{:S(2)}, u32[]{:S(2)}) collective-permute-start(bf16[64,2560]{1,0:T(8,128)(2,1)S(1)} %collective-permute-done.1), channel_id=1, source_target_pairs={{0,4},{1,3},{2,6},{3,1},{4,0},{5,7},{6,2},{7,5},{8,12},{9,11},{10,... | collective-permute-start | bytes 983048 | tf_op jit(solution)/shard_map/ppermute | solution.py:199
  16.5 16.2 %collective-permute-start.5 = (bf16[64,2560]{1,0:T(8,128)(2,1)}, bf16[64,2560]{1,0:T(8,128)(2,1)S(1)}, u32[]{:S(2)}, u32[]{:S(2)}) collective-permute-start(bf16[64,2560]{1,0:T(8,128)(2,1)} %param.12), channel_id=1, source_target_pairs={{0,4},{1,3},{2,6},{3,1},{4,0},{5,7},{6,2},{7,5},{8,12},{9,11},{10,... | collective-permute-start | bytes 983048 | tf_op jit(solution)/shard_map/ppermute | solution.py:199
  20.4 10.0 %collective-permute-start.2 = (bf16[64,2560]{1,0:T(8,128)(2,1)S(1)}, bf16[64,2560]{1,0:T(8,128)(2,1)S(1)}, u32[]{:S(2)}, u32[]{:S(2)}) collective-permute-start(bf16[64,2560]{1,0:T(8,128)(2,1)S(1)} %collective-permute-done.1), channel_id=1, source_target_pairs={{0,8},{1,9},{2,10},{3,11},{4,12},{5,13},{6,14},{7,15},{8,16},{9,17... | collective-permute-start | bytes 983048 | tf_op jit(solution)/shard_map/ppermute | solution.py:199
  25.8 8.0 %collective-permute-start.7 = (f32[16,128]{1,0:T(8,128)S(1)}, f32[16,128]{1,0:T(8,128)S(1)}, u32[]{:S(2)}, u32[]{:S(2)}) collective-permute-start(f32[16,128]{1,0:T(8,128)S(1)} %collective-permute-done.3.table_ref), channel_id=1, source_target_pairs={{0,8},{1,9},{2,10},{3,11},{4,12},{5,13},{6,14},{7,15},{8,16},{9,17... | collective-permute-start | bytes 24584 | tf_op jit(solution)/shard_map/ppermute | solution.py:199
  27.9 10.0 %collective-permute-start.10 = (bf16[72,2560]{1,0:T(8,128)(2,1)S(1)}, bf16[72,2560]{1,0:T(8,128)(2,1)S(1)}, u32[]{:S(2)}, u32[]{:S(2)}) collective-permute-start(bf16[72,2560]{1,0:T(8,128)(2,1)S(1)} %fusion.81), channel_id=1, source_target_pairs={{0,2},{1,5},{2,0},{3,7},{4,6},{5,1},{6,4},{7,3},{8,10},{9,13},{10,... | collective-permute-start | bytes 1105928 | tf_op jit(solution)/shard_map/ppermute | solution.py:199
  30.4 11.3 %collective-permute-start.12 = (bf16[64,2560]{1,0:T(8,128)(2,1)S(1)}, bf16[64,2560]{1,0:T(8,128)(2,1)S(1)}, u32[]{:S(2)}, u32[]{:S(2)}) collective-permute-start(bf16[64,2560]{1,0:T(8,128)(2,1)S(1)} %collective-permute-done.2), channel_id=1, source_target_pairs={{0,4},{1,3},{2,6},{3,1},{4,0},{5,7},{6,2},{7,5},{8,12},{9,11},{10,... | collective-permute-start | bytes 983048 | tf_op jit(solution)/shard_map/ppermute | solution.py:199
  31.8 16.8 %collective-permute-start.9 = (bf16[64,2560]{1,0:T(8,128)(2,1)S(1)}, bf16[64,2560]{1,0:T(8,128)(2,1)S(1)}, u32[]{:S(2)}, u32[]{:S(2)}) collective-permute-start(bf16[64,2560]{1,0:T(8,128)(2,1)S(1)} %collective-permute-done.2), channel_id=1, source_target_pairs={{0,8},{1,9},{2,10},{3,11},{4,12},{5,13},{6,14},{7,15},{8,16},{9,17... | collective-permute-start | bytes 983048 | tf_op jit(solution)/shard_map/ppermute | solution.py:199
  33.9 16.3 %collective-permute-start.8 = (f32[16,128]{1,0:T(8,128)S(1)}, f32[16,128]{1,0:T(8,128)S(1)}, u32[]{:S(2)}, u32[]{:S(2)}) collective-permute-start(f32[16,128]{1,0:T(8,128)S(1)} %collective-permute-done.7.table_ref), channel_id=1, source_target_pairs={{0,8},{1,9},{2,10},{3,11},{4,12},{5,13},{6,14},{7,15},{8,16},{9,17... | collective-permute-start | bytes 24584 | tf_op jit(solution)/shard_map/ppermute | solution.py:199
  34.7 57.9 %collective-permute-start.6 = (bf16[72,2560]{1,0:T(8,128)(2,1)S(1)}, bf16[72,2560]{1,0:T(8,128)(2,1)S(1)}, u32[]{:S(2)}, u32[]{:S(2)}) collective-permute-start(bf16[72,2560]{1,0:T(8,128)(2,1)S(1)} %fusion.83), channel_id=1, source_target_pairs={{0,2},{1,5},{2,0},{3,7},{4,6},{5,1},{6,4},{7,3},{8,10},{9,13},{10,... | collective-permute-start | bytes 1105928 | tf_op jit(solution)/shard_map/ppermute | solution.py:199
  46.9 10.7 %collective-permute-start.13 = (bf16[72,2560]{1,0:T(8,128)(2,1)S(1)}, bf16[72,2560]{1,0:T(8,128)(2,1)S(1)}, u32[]{:S(2)}, u32[]{:S(2)}) collective-permute-start(bf16[72,2560]{1,0:T(8,128)(2,1)S(1)} %fusion.85), channel_id=1, source_target_pairs={{0,2},{1,5},{2,0},{3,7},{4,6},{5,1},{6,4},{7,3},{8,10},{9,13},{10,... | collective-permute-start | bytes 1105928 | tf_op jit(solution)/shard_map/ppermute | solution.py:199
  48.6 12.0 %collective-permute-start.15 = (bf16[64,2560]{1,0:T(8,128)(2,1)S(1)}, bf16[64,2560]{1,0:T(8,128)(2,1)S(1)}, u32[]{:S(2)}, u32[]{:S(2)}) collective-permute-start(bf16[64,2560]{1,0:T(8,128)(2,1)S(1)} %collective-permute-done.9), channel_id=1, source_target_pairs={{0,4},{1,3},{2,6},{3,1},{4,0},{5,7},{6,2},{7,5},{8,12},{9,11},{10,... | collective-permute-start | bytes 983048 | tf_op jit(solution)/shard_map/ppermute | solution.py:199
  51.1 12.5 %collective-permute-start.17 = (bf16[72,2560]{1,0:T(8,128)(2,1)S(1)}, bf16[72,2560]{1,0:T(8,128)(2,1)S(1)}, u32[]{:S(2)}, u32[]{:S(2)}) collective-permute-start(bf16[72,2560]{1,0:T(8,128)(2,1)S(1)} %slice.280), channel_id=1, source_target_pairs={{0,2},{1,5},{2,0},{3,7},{4,6},{5,1},{6,4},{7,3},{8,10},{9,13},{10,... | collective-permute-start | bytes 1105928 | tf_op jit(solution)/shard_map/ppermute | solution.py:199
  62.4 13.4 %collective-permute-start.16 = (bf16[72,2560]{1,0:T(8,128)(2,1)S(1)}, bf16[72,2560]{1,0:T(8,128)(2,1)S(1)}, u32[]{:S(2)}, u32[]{:S(2)}) collective-permute-start(bf16[72,2560]{1,0:T(8,128)(2,1)S(1)} %fusion.87), channel_id=1, source_target_pairs={{0,2},{1,5},{2,0},{3,7},{4,6},{5,1},{6,4},{7,3},{8,10},{9,13},{10,... | collective-permute-start | bytes 1105928 | tf_op jit(solution)/shard_map/ppermute | solution.py:199
  68.3 7.1 %collective-permute-start.18 = (bf16[64,2560]{1,0:T(8,128)(2,1)S(1)}, bf16[64,2560]{1,0:T(8,128)(2,1)S(1)}, u32[]{:S(2)}, u32[]{:S(2)}) collective-permute-start(bf16[64,2560]{1,0:T(8,128)(2,1)S(1)} %fusion.89), channel_id=1, source_target_pairs={{0,4},{1,3},{2,6},{3,1},{4,0},{5,7},{6,2},{7,5},{8,12},{9,11},{10,... | collective-permute-start | bytes 983048 | tf_op jit(solution)/shard_map/ppermute | solution.py:199
  77.7 7.6 %collective-permute-start.22 = (bf16[72,2560]{1,0:T(8,128)(2,1)S(1)}, bf16[72,2560]{1,0:T(8,128)(2,1)S(1)}, u32[]{:S(2)}, u32[]{:S(2)}) collective-permute-start(bf16[72,2560]{1,0:T(8,128)(2,1)S(1)} %slice.282), channel_id=1, source_target_pairs={{0,2},{1,5},{2,0},{3,7},{4,6},{5,1},{6,4},{7,3},{8,10},{9,13},{10,... | collective-permute-start | bytes 1105928 | tf_op jit(solution)/shard_map/ppermute | solution.py:199
  79.7 18.1 %collective-permute-start.26 = (bf16[64,2560]{1,0:T(8,128)(2,1)S(1)}, bf16[64,2560]{1,0:T(8,128)(2,1)S(1)}, u32[]{:S(2)}, u32[]{:S(2)}) collective-permute-start(bf16[64,2560]{1,0:T(8,128)(2,1)S(1)} %fusion.88), channel_id=1, source_target_pairs={{0,8},{1,9},{2,10},{3,11},{4,12},{5,13},{6,14},{7,15},{8,16},{9,17... | collective-permute-start | bytes 983048 | tf_op jit(solution)/shard_map/ppermute | solution.py:199
  88.8 8.5 %collective-permute-start.25 = (bf16[64,2560]{1,0:T(8,128)(2,1)S(1)}, bf16[64,2560]{1,0:T(8,128)(2,1)S(1)}, u32[]{:S(2)}, u32[]{:S(2)}) collective-permute-start(bf16[64,2560]{1,0:T(8,128)(2,1)S(1)} %fusion.90), channel_id=1, source_target_pairs={{0,4},{1,3},{2,6},{3,1},{4,0},{5,7},{6,2},{7,5},{8,12},{9,11},{10,... | collective-permute-start | bytes 983048 | tf_op jit(solution)/shard_map/ppermute | solution.py:199
  91.5 12.4 %collective-permute-start.28 = (bf16[72,2560]{1,0:T(8,128)(2,1)S(1)}, bf16[72,2560]{1,0:T(8,128)(2,1)S(1)}, u32[]{:S(2)}, u32[]{:S(2)}) collective-permute-start(bf16[72,2560]{1,0:T(8,128)(2,1)S(1)} %slice.284), channel_id=1, source_target_pairs={{0,2},{1,5},{2,0},{3,7},{4,6},{5,1},{6,4},{7,3},{8,10},{9,13},{10,... | collective-permute-start | bytes 1105928 | tf_op jit(solution)/shard_map/ppermute | solution.py:199
  93.0 8.1 %collective-permute-start.24 = (bf16[144,2560]{1,0:T(8,128)(2,1)S(1)}, bf16[144,2560]{1,0:T(8,128)(2,1)S(1)}, u32[]{:S(2)}, u32[]{:S(2)}) collective-permute-start(bf16[144,2560]{1,0:T(8,128)(2,1)S(1)} %fusion.64), channel_id=1, source_target_pairs={{0,1},{1,0},{2,3},{3,2},{4,5},{5,4},{6,7},{7,6},{8,9},{9,8},{10,11... | collective-permute-start | bytes 2211848 | tf_op jit(solution)/shard_map/ppermute | solution.py:199
  98.0 16.6 %collective-permute-start.31 = (bf16[64,2560]{1,0:T(8,128)(2,1)S(1)}, bf16[64,2560]{1,0:T(8,128)(2,1)S(1)}, u32[]{:S(2)}, u32[]{:S(2)}) collective-permute-start(bf16[64,2560]{1,0:T(8,128)(2,1)S(1)} %add_convert_fusion.6), channel_id=1, source_target_pairs={{0,8},{1,9},{2,10},{3,11},{4,12},{5,13},{6,14},{7,15},{8,16},{9,17... | collective-permute-start | bytes 983048 | tf_op jit(solution)/shard_map/ppermute | solution.py:199
  104.4 9.6 %collective-permute-start.30 = (bf16[64,2560]{1,0:T(8,128)(2,1)S(1)}, bf16[64,2560]{1,0:T(8,128)(2,1)S(1)}, u32[]{:S(2)}, u32[]{:S(2)}) collective-permute-start(bf16[64,2560]{1,0:T(8,128)(2,1)S(1)} %fusion.91), channel_id=1, source_target_pairs={{0,4},{1,3},{2,6},{3,1},{4,0},{5,7},{6,2},{7,5},{8,12},{9,11},{10,... | collective-permute-start | bytes 983048 | tf_op jit(solution)/shard_map/ppermute | solution.py:199
  106.2 8.9 %collective-permute-start.29 = (bf16[72,2560]{1,0:T(8,128)(2,1)S(1)}, bf16[72,2560]{1,0:T(8,128)(2,1)S(1)}, u32[]{:S(2)}, u32[]{:S(2)}) collective-permute-start(bf16[72,2560]{1,0:T(8,128)(2,1)S(1)} %slice.287), channel_id=1, source_target_pairs={{0,2},{1,5},{2,0},{3,7},{4,6},{5,1},{6,4},{7,3},{8,10},{9,13},{10,... | collective-permute-start | bytes 1105928 | tf_op jit(solution)/shard_map/ppermute | solution.py:199
  116.4 11.5 %collective-permute-start.33 = (bf16[64,2560]{1,0:T(8,128)(2,1)S(1)}, bf16[64,2560]{1,0:T(8,128)(2,1)S(1)}, u32[]{:S(2)}, u32[]{:S(2)}) collective-permute-start(bf16[64,2560]{1,0:T(8,128)(2,1)S(1)} %add_convert_fusion.5), channel_id=1, source_target_pairs={{0,8},{1,9},{2,10},{3,11},{4,12},{5,13},{6,14},{7,15},{8,16},{9,17... | collective-permute-start | bytes 983048 | tf_op jit(solution)/shard_map/ppermute | solution.py:199
  (19 other events, 115.8 us)
